TPU v7x, 128 devices: a whole 4x4x4 slice. The times are simulated.
128 devices in a mesh: left: 16 (over z, x), right: 8 (over y, core).
Axes of the slice: x: 4, y: 4, z: 4, core: 2. Of those that a mesh axis runs over, the one named last changes fastest.
Arguments:
- species: float32 [4, 512, 256, 256], P(None, None, 'left', 'right'), may hold values from -6 to 6
- coupling: float32 [4, 4], replicated, may hold values from -4 to 4
- symbol_x: float32 [512], replicated, may hold values from 0.3 to 3
- symbol_y: float32 [256], replicated, may hold values from 0.3 to 3
- symbol_z: float32 [256], replicated, may hold values from 0.3 to 3
Outputs:
- modes: float32 [4, 512, 256, 256], P(None, 'left', 'right')
All inputs are finite; a program needn't handle non-finite values.
Results may differ from a plain program's by a relative error of at most 0.000071.
Values sent between devices are 32-bit elements; how exact they have to be, the bound alone decides.
A program may use at most 128 MiB of HBM per device.

v0:
```python
import jax
import jax.numpy as jnp
from jax import lax
from jax.sharding import PartitionSpec as P


def basis_table(count):
    rank = jnp.arange(count)
    angle = 2.0 * jnp.pi / count * (rank[:, None] * rank[None, :] % count).astype(jnp.float32)
    return (jnp.cos(angle) + jnp.sin(angle)) * count ** (-0.5)


def along_dim(values, dim):
    moved = jnp.tensordot(
        values, basis_table(values.shape[dim]), axes=([dim], [0]), precision=lax.Precision.HIGHEST
    )
    return jnp.moveaxis(moved, -1, dim)


def body(species, coupling, symbol_x, symbol_y, symbol_z):
    part_values = species
    part_values = along_dim(part_values, 1)
    part_values = lax.all_to_all(part_values, "left", split_axis=1, concat_axis=2, tiled=True)
    part_values = along_dim(part_values, 2)
    pencil_values = part_values
    pencil_values = lax.all_to_all(pencil_values, "right", split_axis=2, concat_axis=3, tiled=True)
    pencil_values = along_dim(pencil_values, 3)
    share_x = pencil_values.shape[1]
    part_x = lax.dynamic_slice_in_dim(symbol_x, lax.axis_index("left") * share_x, share_x)
    share_y = pencil_values.shape[2]
    part_y = lax.dynamic_slice_in_dim(symbol_y, lax.axis_index("right") * share_y, share_y)
    symbol = part_x[:, None, None] + part_y[None, :, None] + symbol_z[None, None, :]
    weight_xyz = 1.0 / (1.0 + symbol)
    mixed_fields = jnp.einsum(
        "ab,bxyz->axyz", coupling, pencil_values, precision=lax.Precision.HIGHEST
    )
    pencil_values = weight_xyz * pencil_values + (1.0 - weight_xyz) * mixed_fields
    return pencil_values


def solution(mesh):
    in_specs = (P(None, None, "left", "right"), P(), P(), P(), P())
    out_specs = P(None, "left", "right", None)
    return jax.shard_map(body, mesh=mesh, in_specs=in_specs, out_specs=out_specs, check_vma=False)
```

profile of v0, /device:TPU:1, one launch (start us, length us, event | category | flops | bytes accessed | tf_op | source)
XLA Modules:
  0.0 341.5 jit_solution(5880469052423909746)
XLA Ops:
  0.0 0.0 copy-start
  0.0 14.5 %fusion.5 = f32[512,2048]{0,1} fusion(f32[512,2048]{0,1:T(8,128)} %bitcast.46), kind=kOutput, calls=%fused_computation.12 | convolution fusion | flops 6446645248 | bytes 8388608
  14.5 14.4 %copy.15 = f32[4,512,16,32]{3,2,0,1:T(8,128)} copy(f32[4,512,16,32]{1,3,2,0:T(8,128)} %bitcast.45) | data formatting | bytes 8388608 | tf_op jit(solution)/shard_map/transpose | solution.py:17
  28.9 16.0 %reshape.41 = f32[16,1,65536]{2,1,0:T(1,128)} reshape(f32[512,4,16,32]{3,2,1,0:T(8,128)} %bitcast.40) | data formatting | bytes 8388608
  44.9 70.5 %all_to_all.36 = f32[16,1,65536]{2,1,0:T(1,128)} all-to-all(f32[16,1,65536]{2,1,0:T(1,128)} %reshape.41), channel_id=1, replica_groups=mesh['left'=16,'right'=8] {'left'}, dimensions={0} | all-to-all | bytes 8388608 | tf_op jit(solution)/shard_map/all_to_all | solution.py:23
  115.4 0.6 broadcast.113
  116.0 14.0 %reduce = f32[16,65536]{1,0:T(8,128)} reduce(f32[16,1,65536]{2,1,0:T(1,128)} %all_to_all.36, f32[]{:T(128)} %broadcast.113), dimensions={1}, to_apply=%all_to_all.26.reduce_sub_computation | reduce | bytes 8388612 | tf_op jit(solution)/shard_map/all_to_all | solution.py:23
  130.1 15.1 %reshape.42 = f32[512,4,16,32]{3,2,1,0:T(8,128)} reshape(f32[16,65536]{1,0:T(8,128)} %reduce) | data formatting | bytes 8388608
  145.1 7.1 %copy.16 = f32[4,16,32,16,32]{4,3,1,2,0:T(8,128)S(1)} copy(f32[4,16,32,16,32]{4,3,0,2,1:T(8,128)} %bitcast.42) | data formatting | bytes 8388608 | tf_op jit(solution)/shard_map/all_to_all | solution.py:23
  152.3 30.0 %convolution_bitcast_fusion = f32[4,32,256,32]{2,3,1,0:T(8,128)} fusion(f32[4,32,256,32]{3,2,1,0:T(8,128)S(1)} %bitcast.39), kind=kOutput, calls=%fused_computation.5 | convolution fusion | flops 3222274048 | bytes 8388608 | tf_op jit(solution)/shard_map/dot_general | solution.py:14
  182.3 14.4 %copy.18 = f32[4,32,256,32]{3,1,0,2:T(8,128)} copy(f32[4,32,256,32]{2,3,1,0:T(8,128)} %convolution_bitcast_fusion) | data formatting | bytes 8388608 | tf_op jit(solution)/shard_map/transpose | solution.py:17
  196.7 12.8 %reshape.43 = f32[8,1,131072]{2,1,0:T(1,128)} reshape(f32[256,4,32,32]{3,2,1,0:T(8,128)} %bitcast.41) | data formatting | bytes 8388608
  209.5 0.0 copy-start.2
  209.5 0.0 copy-start.1
  209.5 7.1 %all-to-all-start.1 = ((f32[8,1,131072]{2,1,0:T(1,128)}), f32[8,1,131072]{2,1,0:T(1,128)}, u32[]{:S(2)}, u32[]{:S(2)}) async-start(f32[8,1,131072]{2,1,0:T(1,128)} %reshape.43), calls=%async_computation.1 | async-start | bytes 8388608 | tf_op jit(solution)/shard_map/all_to_all | solution.py:26
  216.7 0.0 copy-done.2
  216.7 0.1 dynamic_slice.7
  216.7 0.8 dynamic_slice.6
  217.5 0.1 broadcast_add_fusion
  217.6 0.0 copy-done.1
  217.6 0.2 add_divide_fusion
  217.8 47.6 %all-to-all-done.1 = f32[8,1,131072]{2,1,0:T(1,128)} async-done(((f32[8,1,131072]{2,1,0:T(1,128)}), f32[8,1,131072]{2,1,0:T(1,128)}, u32[]{:S(2)}, u32[]{:S(2)}) %all-to-all-start.1) | async-done | bytes 4194336 | tf_op jit(solution)/shard_map/all_to_all | solution.py:26
  265.4 13.8 %reduce.1 = f32[8,131072]{1,0:T(8,128)} reduce(f32[8,1,131072]{2,1,0:T(1,128)} %all-to-all-done.1, f32[]{:T(128)} %broadcast.113), dimensions={1}, to_apply=%all_to_all.30.reduce_sub_computation | reduce | bytes 8388612 | tf_op jit(solution)/shard_map/all_to_all | solution.py:26
  279.2 13.3 %reshape.44 = f32[256,4,32,32]{3,2,1,0:T(8,128)} reshape(f32[8,131072]{1,0:T(8,128)} %reduce.1) | data formatting | bytes 8388608
  292.5 17.8 %copy.31 = f32[4,32,8,32,32]{4,2,3,1,0:T(8,128)} copy(f32[4,32,8,32,32]{4,1,0,3,2:T(8,128)} %bitcast.43) | data formatting | bytes 8388608 | tf_op jit(solution)/shard_map/all_to_all | solution.py:26
  310.3 12.3 %all_to_all.33 = f32[4,32,32,256]{3,2,1,0:T(8,128)} reshape(f32[4,32,32,8,32]{4,3,2,1,0:T(8,128)} %bitcast.44) | data formatting | bytes 8388608 | tf_op jit(solution)/shard_map/all_to_all | solution.py:26
  322.6 6.8 %fusion.24 = f32[4,32,32,256]{3,2,1,0:T(8,128)S(1)} fusion(f32[4,32,32,256]{3,2,1,0:T(8,128)} %all_to_all.33), kind=kOutput, calls=%fused_computation.33 | convolution fusion | flops 3222274048 | bytes 8388608 | tf_op jit(solution)/shard_map/dot_general | solution.py:14
  329.4 0.0 copy-done
  329.4 8.5 %fusion = f32[32,32,256,4]{2,3,1,0:T(4,128)S(1)} fusion(f32[4,32,32,256]{3,2,1,0:T(8,128)S(1)} %fusion.24, f32[4,4]{1,0:T(4,128)S(1)} %copy-done), kind=kOutput, calls=%fused_computation.3 | convolution fusion | flops 50331648 | bytes 8388672 | tf_op jit(solution)/shard_map/ab,bxyz->axyz/dot_general | solution.py:34
  338.0 3.3 bitcast_add_fusion
Async XLA Ops:
  0.0 329.4 %copy-start = (f32[4,4]{1,0:T(4,128)S(1)}, f32[4,4]{1,0:T(4,128)}, u32[]{:S(2)}) copy-start(f32[4,4]{1,0:T(4,128)} %param.6) | copy-start | bytes 196
  209.5 7.1 %copy-start.2 = (f32[256]{0:T(256)S(1)}, f32[256]{0:T(256)}, u32[]{:S(2)}) copy-start(f32[256]{0:T(256)} %param.8) | copy-start | bytes 3076
  209.5 8.0 %copy-start.1 = (f32[256]{0:T(256)S(1)}, f32[256]{0:T(256)}, u32[]{:S(2)}) copy-start(f32[256]{0:T(256)} %param.9) | copy-start | bytes 3076
  209.5 55.8 %all-to-all-start.1 = ((f32[8,1,131072]{2,1,0:T(1,128)}), f32[8,1,131072]{2,1,0:T(1,128)}, u32[]{:S(2)}, u32[]{:S(2)}) async-start(f32[8,1,131072]{2,1,0:T(1,128)} %reshape.43), calls=%async_computation.1 | async-start | bytes 8388608 | tf_op jit(solution)/shard_map/all_to_all | solution.py:26
where the time goes:
time: 342 us; the launch traced here: 341 us
  local copies, waits for them, and re-layouts  125 us (37%)
  blocking collectives  70.5 us (21%)
  matrix products  59.8 us (17%)
  waiting for transfers between devices  47.6 us (14%)
  other arithmetic  31.4 us (9%)
  starting transfers between devices  7.11 us (2%)
    all_to_all x1, blocking collectives, body(): lax.all_to_all(part_values, 'left', split_axis=1, concat_axis=2, tiled=True)  70.5 us
    unnamed x10, local copies, waits for them, and re-layouts  57.2 us
    all_to_all x1, waiting for transfers between devices, body(): lax.all_to_all(pencil_values, 'right', split_axis=2, concat_axis=3, tiled...  47.6 us
    dot_general x2, matrix products, along_dim(): jnp.tensordot(values, basis_table(values.shape[dim]), axes=([dim], [0]),...  36.8 us
    all_to_all x2, local copies, waits for them, and re-layouts, body(): lax.all_to_all(pencil_values, 'right', split_axis=2, concat_axis=3, tiled...  30.1 us
    transpose x2, local copies, waits for them, and re-layouts, along_dim(): return jnp.moveaxis(moved, -1, dim)  28.9 us
    unnamed x1, matrix products  14.5 us
    all_to_all x1, other arithmetic, body(): lax.all_to_all(part_values, 'left', split_axis=1, concat_axis=2, tiled=True)  14 us
  transfers between devices with their start and end apart: 1, of which 1 were waited for; matrix products, arithmetic and copies ran while one was open for 0% of the time, Pallas kernels for 0%

commit v1 on v0

v1 whole, which is shorter than its diff:
```python
import jax
import jax.numpy as jnp
import numpy as np
from jax import lax
from jax.experimental import pallas as pl
from jax.experimental.pallas import tpu as pltpu
from jax.sharding import PartitionSpec as P

MESH = pl.DeviceIdType.MESH
F = 4
BLOCKS = 4

LEFT_STEPS = [(dz, dx) for dx in (0, 1, 3, 2) for dz in (1, 3, 2, 0) if (dz, dx) != (0, 0)]
RIGHT_STEPS = [(dy, dc) for dy in (1, 3, 2, 0) for dc in (0, 1) if (dy, dc) != (0, 0)]


def basis_table(count):
    rank = np.arange(count)
    angle = 2.0 * np.pi / count * (rank[:, None] * rank[None, :] % count)
    return ((np.cos(angle) + np.sin(angle)) * count**-0.5).astype(np.float32)


def halves(table):
    high = table.astype(jnp.bfloat16)
    low = (table - high.astype(np.float32)).astype(jnp.bfloat16)
    return high, low


def split(values):
    high = values.astype(jnp.bfloat16)
    return high, (values - high.astype(jnp.float32)).astype(jnp.bfloat16)


def dot_nt(a, b):
    return lax.dot_general(a, b, (((1,), (1,)), ((), ())), preferred_element_type=jnp.float32)


def dot_nn(a, b):
    return lax.dot_general(a, b, (((1,), (0,)), ((), ())), preferred_element_type=jnp.float32)


def exchange_blocks(arrays, width):
    lane = lax.broadcasted_iota(jnp.int32, arrays[0].shape, 1)
    arrays = list(arrays)
    bit = 1
    while bit < len(arrays):
        upper = (lane // width) % (2 * bit) >= bit
        for i in range(len(arrays)):
            if i & bit == 0:
                a, b = arrays[i], arrays[i + bit]
                arrays[i] = jnp.where(upper, pltpu.roll(b, width * bit, 1), a)
                arrays[i + bit] = jnp.where(upper, b, pltpu.roll(a, 128 - width * bit, 1))
        bit *= 2
    return arrays


def kernel(
    species, hx_high_hbm, hx_low_hbm, h_high_hbm, h_low_hbm, out,
    grid, hx_high, hx_low, h_high, h_low, d_high, d_low, s1, r1, d2, e_high, e_low, s2, r2, g_high, g_low, modes,
    in_sem, h_sem, send1, recv1, send2, recv2, out_sem,
):
    left, right = lax.axis_index("left"), lax.axis_index("right")
    z, x = left // 4, left % 4
    y, core = right // 2, right % 2
    left_peers = [lax.rem(z + dz, 4) * 4 + lax.rem(x + dx, 4) for dz, dx in LEFT_STEPS]
    right_peers = [lax.rem(y + dy, 4) * 2 + lax.rem(core + dc, 2) for dy, dc in RIGHT_STEPS]

    barrier = pltpu.get_barrier_semaphore()
    for peer in left_peers:
        pl.semaphore_signal(barrier, inc=1, device_id=(peer, right), device_id_type=MESH)
    for peer in right_peers:
        pl.semaphore_signal(barrier, inc=1, device_id=(left, peer), device_id_type=MESH)

    def load(f, t):
        return pltpu.make_async_copy(
            species.at[pl.ds(512 * f, 512), pl.ds(128 * t, 128)],
            grid.at[pl.ds((4 * f + t) * 512, 512)],
            in_sem.at[f, t],
        )

    for f in range(F):
        for t in range(4):
            load(f, t).start()
        if f == 0:
            tables = [
                pltpu.make_async_copy(a, b, h_sem.at[i])
                for i, (a, b) in enumerate(
                    [(hx_high_hbm, hx_high), (hx_low_hbm, hx_low), (h_high_hbm, h_high), (h_low_hbm, h_low)]
                )
            ]
            for table in tables:
                table.start()

    def first(f, b, k):
        return pltpu.make_async_remote_copy(
            src_ref=s1.at[f, b, left_peers[k]],
            dst_ref=r1.at[f, b, left],
            send_sem=send1.at[f, b],
            recv_sem=recv1.at[f, b],
            device_id=(left_peers[k], right),
            device_id_type=MESH,
        )

    def second(f, b, k):
        return pltpu.make_async_remote_copy(
            src_ref=s2.at[f, b, right_peers[k]],
            dst_ref=r2.at[f, b, right],
            send_sem=send2.at[f, b],
            recv_sem=recv2.at[f, b],
            device_id=(left, right_peers[k]),
            device_id_type=MESH,
        )

    def all_first(f, b):
        return pltpu.make_async_remote_copy(
            src_ref=s1.at[f, b, pl.ds(0, 15)],
            dst_ref=r1.at[f, b, pl.ds(0, 15)],
            send_sem=send1.at[f, b],
            recv_sem=recv1.at[f, b],
            device_id=(left_peers[0], right),
            device_id_type=MESH,
        )

    def all_second(f, b):
        return pltpu.make_async_remote_copy(
            src_ref=s2.at[f, b, pl.ds(0, 7)],
            dst_ref=r2.at[f, b, pl.ds(0, 7)],
            send_sem=send2.at[f, b],
            recv_sem=recv2.at[f, b],
            device_id=(left, right_peers[0]),
            device_id_type=MESH,
        )

    def along_x(f, opening):
        for t in range(4):
            load(f, t).wait()
        for t in range(4):
            for zi in range(32):
                rows = grid[pl.ds((4 * f + t) * 512 + zi, 16, stride=32), :]
                high, low = split(rows)
                d_high[pl.ds(16 * zi, 16), pl.ds(128 * t, 128)] = high
                d_low[pl.ds(16 * zi, 16), pl.ds(128 * t, 128)] = low
        if opening:
            for table in tables:
                table.wait()

        def block(b, carry):
            rows = pl.ds(pl.multiple_of(128 * b, 128), 128)
            part = dot_nt(hx_high[rows, :], d_high[...])
            part += dot_nt(hx_high[rows, :], d_low[...])
            part += dot_nt(hx_low[rows, :], d_high[...])
            s1[f, b] = part.reshape(16, 8, 512)
            r1[f, b, left] = s1[f, b, left]
            if opening:

                @pl.when(b == 0)
                def _():
                    pl.semaphore_wait(barrier, len(left_peers) + len(right_peers))

            for k in range(len(left_peers)):
                first(f, b, k).start()
            return carry

        lax.fori_loop(0, BLOCKS, block, 0)

    def along_y(f, b):
        all_first(f, b).wait_recv()
        for t in range(4):
            for g in range(2):
                arrays = [r1[f, b, 8 * g + i, :, pl.ds(128 * t, 128)] for i in range(8)]
                for i, array in enumerate(exchange_blocks(arrays, 16)):
                    d2[pl.ds(256 * g + 8 * (8 * t + i), 8), :] = array
        for g in range(2):
            for kx in range(8):
                high, low = split(d2[pl.ds(256 * g + kx, 32, stride=8), :])
                e_high[pl.ds(32 * kx, 32), pl.ds(128 * g, 128)] = high
                e_low[pl.ds(32 * kx, 32), pl.ds(128 * g, 128)] = low
        part = dot_nt(h_high[...], e_high[...])
        part += dot_nt(h_high[...], e_low[...])
        part += dot_nt(h_low[...], e_high[...])
        s2[f, b] = part.reshape(8, 32, 256)
        r2[f, b, right] = s2[f, b, right]
        for k in range(len(right_peers)):
            second(f, b, k).start()

    def store(f, b):
        return pltpu.make_async_copy(
            modes.at[f, pl.ds(8 * b, 8)], out.at[f, pl.ds(8 * b, 8)], out_sem.at[f, b]
        )

    def along_z(f, b):
        all_second(f, b).wait_recv()
        for t in range(2):
            for g in range(2):
                arrays = [r2[f, b, 4 * g + i, :, pl.ds(128 * t, 128)] for i in range(4)]
                for i, array in enumerate(exchange_blocks(arrays, 32)):
                    high, low = split(array)
                    g_high[pl.ds(32 * (4 * t + i), 32), pl.ds(128 * g, 128)] = high
                    g_low[pl.ds(32 * (4 * t + i), 32), pl.ds(128 * g, 128)] = low
        part = dot_nn(g_high[...], h_high[...])
        part += dot_nn(g_low[...], h_high[...])
        part += dot_nn(g_high[...], h_low[...])
        modes[f, pl.ds(8 * b, 8)] = part.reshape(8, 32, 256)
        store(f, b).start()

    along_x(0, True)

    def field(f, carry):
        @pl.when(f < F - 1)
        def _():
            along_x(f + 1, False)

        def block(b, inner):
            along_y(f, b)
            step = BLOCKS * f + b - 1

            @pl.when(step >= 0)
            def _():
                along_z(step // BLOCKS, step % BLOCKS)

            return inner

        return lax.fori_loop(0, BLOCKS, block, carry)

    lax.fori_loop(0, F, field, 0)
    along_z(F - 1, BLOCKS - 1)

    def finish(step, carry):
        f, b = step // BLOCKS, step % BLOCKS
        all_first(f, b).wait_send()
        all_second(f, b).wait_send()
        store(f, b).wait()
        return carry

    lax.fori_loop(0, F * BLOCKS, finish, 0)


def transform(species):
    any_space = pl.BlockSpec(memory_space=pl.ANY)
    wide = basis_table(512)
    rows = np.arange(512).reshape(16, BLOCKS, 8).transpose(1, 0, 2).reshape(-1)
    hx_high, hx_low = halves(wide[rows])
    h_high, h_low = halves(basis_table(256))
    flat = jnp.transpose(species, (0, 2, 3, 1)).reshape(F * 512, 512)
    return pl.pallas_call(
        kernel,
        out_shape=jax.ShapeDtypeStruct((F, 32, 32, 256), jnp.float32),
        in_specs=[any_space] * 5,
        out_specs=any_space,
        scratch_shapes=[
            pltpu.VMEM((F * 4 * 512, 128), jnp.float32),
            pltpu.VMEM((512, 512), jnp.bfloat16),
            pltpu.VMEM((512, 512), jnp.bfloat16),
            pltpu.VMEM((256, 256), jnp.bfloat16),
            pltpu.VMEM((256, 256), jnp.bfloat16),
            pltpu.VMEM((512, 512), jnp.bfloat16),
            pltpu.VMEM((512, 512), jnp.bfloat16),
            pltpu.VMEM((F, BLOCKS, 16, 8, 512), jnp.float32),
            pltpu.VMEM((F, BLOCKS, 16, 8, 512), jnp.float32),
            pltpu.VMEM((512, 128), jnp.float32),
            pltpu.VMEM((256, 256), jnp.bfloat16),
            pltpu.VMEM((256, 256), jnp.bfloat16),
            pltpu.VMEM((F, BLOCKS, 8, 32, 256), jnp.float32),
            pltpu.VMEM((F, BLOCKS, 8, 32, 256), jnp.float32),
            pltpu.VMEM((256, 256), jnp.bfloat16),
            pltpu.VMEM((256, 256), jnp.bfloat16),
            pltpu.VMEM((F, 32, 32, 256), jnp.float32),
            pltpu.SemaphoreType.DMA((F, 4)),
            pltpu.SemaphoreType.DMA((4,)),
            pltpu.SemaphoreType.DMA((F, BLOCKS)),
            pltpu.SemaphoreType.DMA((F, BLOCKS)),
            pltpu.SemaphoreType.DMA((F, BLOCKS)),
            pltpu.SemaphoreType.DMA((F, BLOCKS)),
            pltpu.SemaphoreType.DMA((F, BLOCKS)),
        ],
        compiler_params=pltpu.CompilerParams(
            collective_id=0, has_side_effects=True, vmem_limit_bytes=48 * 2**20
        ),
        name="transform",
    )(flat, hx_high, hx_low, h_high, h_low)


def body(species, coupling, symbol_x, symbol_y, symbol_z):
    modes = transform(species)
    part_x = lax.dynamic_slice_in_dim(symbol_x, lax.axis_index("left") * 32, 32)
    part_y = lax.dynamic_slice_in_dim(symbol_y, lax.axis_index("right") * 32, 32)
    symbol = part_x[:, None, None] + part_y[None, :, None] + symbol_z[None, None, :]
    weight = 1.0 / (1.0 + symbol)
    fields = []
    for a in range(F):
        mixed = sum(coupling[a, b] * modes[b] for b in range(F))
        fields.append(weight * modes[a] + (1.0 - weight) * mixed)
    return jnp.stack(fields)


def solution(mesh):
    in_specs = (P(None, None, "left", "right"), P(), P(), P(), P())
    out_specs = P(None, "left", "right", None)
    return jax.shard_map(body, mesh=mesh, in_specs=in_specs, out_specs=out_specs, check_vma=False)
```

time: 342 us -> 102 us (0.30)
  local copies, waits for them, and re-layouts: 125 us -> 7.37 us
  Pallas kernels: 0 us -> 79.9 us
  blocking collectives: 70.5 us -> 0 us
  matrix products: 59.8 us -> 0 us
  waiting for transfers between devices: 47.6 us -> 0 us
  other arithmetic: 31.4 us -> 14 us
  starting transfers between devices: 7.11 us -> 0 us
    pallas_call x0 -> x1, Pallas kernels: none -> 79.9 us  [transform(): pl.pallas_call(kernel, out_shape=jax.ShapeDtypeStruct((F, 32, 32, 256), j...]
    all_to_all x1 -> x0, blocking collectives: 70.5 us -> none  [body(): lax.all_to_all(part_values, 'left', split_axis=1, concat_axis=2, tiled=True)]
    unnamed x10, local copies, waits for them, and re-layouts: 57.2 us -> 3.89 us
    all_to_all x1 -> x0, waiting for transfers between devices: 47.6 us -> none  [body(): lax.all_to_all(pencil_values, 'right', split_axis=2, concat_axis=3, tiled...]
    dot_general x3 -> x0, matrix products: 45.3 us -> none  [the longest x2 36.8 us: along_dim(): jnp.tensordot(values, basis_table(values.shape[dim]), axes=([dim], [0]),...]
    all_to_all x4 -> x0, local copies, waits for them, and re-layouts: 37.8 us -> none  [the longest x2 30.1 us: body(): lax.all_to_all(pencil_values, 'right', split_axis=2, concat_axis=3, tiled...]
    transpose x2 -> x0, local copies, waits for them, and re-layouts: 28.9 us -> none  [along_dim(): return jnp.moveaxis(moved, -1, dim)]
    all_to_all x2 -> x0, other arithmetic: 27.8 us -> none  [the longest x1 14 us: body(): lax.all_to_all(part_values, 'left', split_axis=1, concat_axis=2, tiled=True)]
  transfers between devices with their start and end apart: 1 -> 0, of which waited for: 1 -> 0; matrix products, arithmetic and copies ran while one was open for 0% -> 0% of each run, Pallas kernels for 0% -> 0%
where the time goes in v1:
time: 102 us; the launch traced here: 101 us
  Pallas kernels  79.9 us (78%)
  other arithmetic  14 us (14%)
  local copies, waits for them, and re-layouts  7.37 us (7%)
    pallas_call x1, Pallas kernels, transform(): pl.pallas_call(kernel, out_shape=jax.ShapeDtypeStruct((F, 32, 32, 256), j...  79.9 us
    add x2, other arithmetic, body(): fields.append(weight * modes[a] + (1.0 - weight) * mixed)  11.6 us
    unnamed x10, local copies, waits for them, and re-layouts  3.89 us
    another operation x1, other arithmetic, body(): return jnp.stack(fields)  2.33 us

profile of v1, /device:TPU:1, one launch (start us, length us, event | category | flops | bytes accessed | tf_op | source)
XLA Modules:
  0.0 101.4 jit_solution(4727067328097754690)
XLA Ops:
  0.0 0.8 dynamic_slice.6
  0.8 0.8 dynamic_slice.7
  1.5 0.1 broadcast_add_fusion
  1.6 2.0 %fusion = (f32[1,1]{1,0:T(1,128)}, f32[1,1]{1,0:T(1,128)}, f32[1,1]{1,0:T(1,128)}, f32[1,1]{1,0:T(1,128)}, f32[1,1]{1,0:T(1,128)}, /*index=5*/f32[1,1]{1,0:T(1,1...) fusion(f32[4,4]{1,0:T(4,128)} %param.10), kind=kLoop, calls=%fused_computation.7 | loop fusion | bytes 128 | tf_op jit(solution)/shard_map/slice | solution.py:291
  3.6 0.0 copy-start
  3.6 1.0 %copy-done = bf16[512,512]{1,0:T(8,128)(2,1)S(1)} copy-done((bf16[512,512]{1,0:T(8,128)(2,1)S(1)}, bf16[512,512]{1,0:T(8,128)(2,1)}, u32[]{:S(2)}) %copy-start) | copy-done | bytes 524312
  4.6 0.0 copy-start.1
  4.6 1.0 %copy-done.1 = bf16[512,512]{1,0:T(8,128)(2,1)S(1)} copy-done((bf16[512,512]{1,0:T(8,128)(2,1)S(1)}, bf16[512,512]{1,0:T(8,128)(2,1)}, u32[]{:S(2)}) %copy-start.1) | copy-done | bytes 524312
  5.6 0.0 copy-start.2
  5.6 0.9 copy-done.2
  6.6 0.0 copy-start.3
  6.6 0.9 copy-done.3
  7.5 0.0 copy-start.4
  7.5 79.9 %transform.1 = f32[4,32,32,256]{3,2,1,0:T(8,128)S(1)} custom-call(f32[2048,512]{1,0:T(8,128)} %bitcast.19, bf16[512,512]{1,0:T(8,128)(2,1)S(1)} %copy-done, bf16[512,512]{1,0:T(8,128)(2,1)S(1)} %copy-done.1, bf16[256,256]{1,0:T(8,128)(2,1)S(1)} %copy-done.2, bf16[256,256]{1,0:T(8,128)(2,1)S(1)} %copy-done.3), custom_call_target="tpu_custom_call" | custom-call | tf_op jit(solution)/shard_map/transform/pallas_call | solution.py:245
  87.4 0.0 copy-done.4
  87.4 5.8 %multiply_add_fusion.3 = (f32[1,32,32,256]{3,2,1,0:T(8,128)S(1)}, f32[1,32,32,256]{3,2,1,0:T(8,128)S(1)}) fusion(f32[4,32,32,256]{3,2,1,0:T(8,128)S(1)} %transform.1, f32[]{:T(128)} %bitcast.5, f32[]{:T(128)} %bitcast.4, f32[]{:T(128)} %bitcast.3, f32[]{:T(128)} %bitcast.2, f32[256]{0:T(256)S(1)} %copy-done.4, f32[32,32]{1,0:T(8,128)S(1)} %broadcast_add_fusion, ...), kind=kLoop, calls=%fused_computation.4 | loop fusion | flops 6291456 | bytes 6296608 | tf_op jit(solution)/shard_map/add | solution.py:292
  93.3 5.8 %multiply_add_fusion.1 = (f32[1,32,32,256]{3,2,1,0:T(8,128)S(1)}, f32[1,32,32,256]{3,2,1,0:T(8,128)S(1)}) fusion(f32[4,32,32,256]{3,2,1,0:T(8,128)S(1)} %transform.1, f32[]{:T(128)} %bitcast.13, f32[]{:T(128)} %bitcast.12, f32[]{:T(128)} %bitcast.11, f32[]{:T(128)} %bitcast.10, f32[256]{0:T(256)S(1)} %copy-done.4, f32[32,32]{1,0:T(8,128)S(1)} %broadcast_add_fusion, ...), kind=kLoop, calls=%fused_computation.2 | loop fusion | flops 6291456 | bytes 6296608 | tf_op jit(solution)/shard_map/add | solution.py:292
  99.0 2.3 %pad_maximum_fusion = f32[4,32,32,256]{3,2,1,0:T(8,128)} fusion(f32[1,32,32,256]{3,2,1,0:T(8,128)S(1)} %get-tuple-element.8, f32[1,32,32,256]{3,2,1,0:T(8,128)S(1)} %get-tuple-element.7, f32[1,32,32,256]{3,2,1,0:T(8,128)S(1)} %get-tuple-element.6, f32[1,32,32,256]{3,2,1,0:T(8,128)S(1)} %get-tuple-element.5), kind=kLoop, calls=%fused_computation | loop fusion | flops 3145728 | bytes 8388608 | tf_op jit(solution)/shard_map/stack | solution.py:293
Async XLA Ops:
  3.6 1.0 %copy-start = (bf16[512,512]{1,0:T(8,128)(2,1)S(1)}, bf16[512,512]{1,0:T(8,128)(2,1)}, u32[]{:S(2)}) copy-start(bf16[512,512]{1,0:T(8,128)(2,1)} %constant.27.clone.hx_high_hbm) | copy-start | bytes 1572868
  4.6 1.0 %copy-start.1 = (bf16[512,512]{1,0:T(8,128)(2,1)S(1)}, bf16[512,512]{1,0:T(8,128)(2,1)}, u32[]{:S(2)}) copy-start(bf16[512,512]{1,0:T(8,128)(2,1)} %constant.28.clone.hx_low_hbm) | copy-start | bytes 1572868
  5.6 0.9 copy-start.2
  6.6 0.9 copy-start.3
  7.5 80.0 %copy-start.4 = (f32[256]{0:T(256)S(1)}, f32[256]{0:T(256)}, u32[]{:S(2)}) copy-start(f32[256]{0:T(256)} %param.13) | copy-start | bytes 3076

commit v2 on v1

v2 whole, which is shorter than its diff:
```python
import jax
import jax.numpy as jnp
import numpy as np
from jax import lax
from jax.experimental import pallas as pl
from jax.experimental.pallas import tpu as pltpu
from jax.sharding import PartitionSpec as P

MESH = pl.DeviceIdType.MESH
F = 4
BLOCKS = 4
LAG = 2

LEFT_STEPS = [(dz, dx) for dx in (0, 1, 3, 2) for dz in (1, 3, 2, 0) if (dz, dx) != (0, 0)]
RIGHT_STEPS = [(dy, dc) for dy in (1, 3, 2, 0) for dc in (0, 1) if (dy, dc) != (0, 0)]


def basis_table(count):
    rank = np.arange(count)
    angle = 2.0 * np.pi / count * (rank[:, None] * rank[None, :] % count)
    return ((np.cos(angle) + np.sin(angle)) * count**-0.5).astype(np.float32)


def halves(table):
    high = table.astype(jnp.bfloat16)
    low = (table - high.astype(np.float32)).astype(jnp.bfloat16)
    return high, low


def split(values):
    high = values.astype(jnp.bfloat16)
    return high, (values - high.astype(jnp.float32)).astype(jnp.bfloat16)


def dot_nt(a, b):
    return lax.dot_general(a, b, (((1,), (1,)), ((), ())), preferred_element_type=jnp.float32)


def dot_nn(a, b):
    return lax.dot_general(a, b, (((1,), (0,)), ((), ())), preferred_element_type=jnp.float32)


def exchange_blocks(arrays, width):
    lane = lax.broadcasted_iota(jnp.int32, arrays[0].shape, 1)
    arrays = list(arrays)
    bit = 1
    while bit < len(arrays):
        upper = (lane // width) % (2 * bit) >= bit
        for i in range(len(arrays)):
            if i & bit == 0:
                a, b = arrays[i], arrays[i + bit]
                arrays[i] = jnp.where(upper, pltpu.roll(b, width * bit, 1), a)
                arrays[i + bit] = jnp.where(upper, b, pltpu.roll(a, 128 - width * bit, 1))
        bit *= 2
    return arrays


def kernel(
    species, tables_x, tables, coupling, symbol_x, symbol_y, symbol_z, out,
    grid, hx, h, d_high, d_low, s1, r1, d2, e_high, e_low, s2, r2, g_high, g_low, modes, base, mix, sx, sy, sz,
    in_sem, h_sem, send1, recv1, send2, recv2,
):
    left, right = lax.axis_index("left"), lax.axis_index("right")
    z, x = left // 4, left % 4
    y, core = right // 2, right % 2
    left_peers = [lax.rem(z + dz, 4) * 4 + lax.rem(x + dx, 4) for dz, dx in LEFT_STEPS]
    right_peers = [lax.rem(y + dy, 4) * 2 + lax.rem(core + dc, 2) for dy, dc in RIGHT_STEPS]

    def load(f, t):
        return pltpu.make_async_copy(
            species.at[pl.ds(512 * f, 512), pl.ds(128 * t, 128)],
            grid.at[pl.ds((4 * f + t) * 512, 512)],
            in_sem.at[f, t],
        )

    small = [
        pltpu.make_async_copy(a, b, h_sem.at[i])
        for i, (a, b) in enumerate(
            [(tables_x, hx), (tables, h), (coupling, mix), (symbol_x, sx), (symbol_y, sy), (symbol_z, sz)]
        )
    ]
    for t in range(4):
        load(0, t).start()
    small[0].start()
    for f in range(1, F):
        for t in range(4):
            load(f, t).start()
    for copy in small[1:]:
        copy.start()

    barrier = pltpu.get_barrier_semaphore()
    for peer in left_peers:
        pl.semaphore_signal(barrier, inc=1, device_id=(peer, right), device_id_type=MESH)
    for peer in right_peers:
        pl.semaphore_signal(barrier, inc=1, device_id=(left, peer), device_id_type=MESH)

    def first(f, b, k):
        return pltpu.make_async_remote_copy(
            src_ref=s1.at[f, b, left_peers[k]],
            dst_ref=r1.at[f, b, left],
            send_sem=send1.at[f, b],
            recv_sem=recv1.at[f, b],
            device_id=(left_peers[k], right),
            device_id_type=MESH,
        )

    def second(f, b, k):
        return pltpu.make_async_remote_copy(
            src_ref=s2.at[f, b, right_peers[k]],
            dst_ref=r2.at[f, b, right],
            send_sem=send2.at[f, b],
            recv_sem=recv2.at[f, b],
            device_id=(left, right_peers[k]),
            device_id_type=MESH,
        )

    def all_first(f, b):
        return pltpu.make_async_remote_copy(
            src_ref=s1.at[f, b, pl.ds(0, 15)],
            dst_ref=r1.at[f, b, pl.ds(0, 15)],
            send_sem=send1.at[f, b],
            recv_sem=recv1.at[f, b],
            device_id=(left_peers[0], right),
            device_id_type=MESH,
        )

    def all_second(f, b):
        return pltpu.make_async_remote_copy(
            src_ref=s2.at[f, b, pl.ds(0, 7)],
            dst_ref=r2.at[f, b, pl.ds(0, 7)],
            send_sem=send2.at[f, b],
            recv_sem=recv2.at[f, b],
            device_id=(left, right_peers[0]),
            device_id_type=MESH,
        )

    def send_first(f, b):
        for k in range(len(left_peers)):
            first(f, b, k).start()

    def along_x(f, carry):
        for t in range(4):
            load(f, t).wait()
        for t in range(4):
            for zi in range(32):
                rows = grid[pl.ds((4 * f + t) * 512 + zi, 16, stride=32), :]
                high, low = split(rows)
                d_high[pl.ds(16 * zi, 16), pl.ds(128 * t, 128)] = high
                d_low[pl.ds(16 * zi, 16), pl.ds(128 * t, 128)] = low

        @pl.when(f == 0)
        def _():
            small[0].wait()

        def pair(p, inner):
            rows = pl.ds(pl.multiple_of(256 * p, 256), 256)
            part = dot_nt(hx[0, rows, :], d_high[...])
            part += dot_nt(hx[0, rows, :], d_low[...])
            part += dot_nt(hx[1, rows, :], d_high[...])
            s1[f, pl.ds(2 * p, 2)] = part.reshape(2, 16, 8, 512)
            for i in range(2):
                r1[f, 2 * p + i, left] = s1[f, 2 * p + i, left]

            @pl.when(p == 0)
            def _():
                @pl.when(f == 0)
                def _():
                    pl.semaphore_wait(barrier, len(left_peers) + len(right_peers))

                send_first(f, 0)

            return inner

        return lax.fori_loop(0, BLOCKS // 2, pair, carry)

    def along_y(f, b):
        all_first(f, b).wait_recv()
        for t in range(4):
            for g in range(2):
                arrays = [r1[f, b, 8 * g + i, :, pl.ds(128 * t, 128)] for i in range(8)]
                for i, array in enumerate(exchange_blocks(arrays, 16)):
                    d2[pl.ds(256 * g + 8 * (8 * t + i), 8), :] = array
        for g in range(2):
            for kx in range(8):
                high, low = split(d2[pl.ds(256 * g + kx, 32, stride=8), :])
                e_high[pl.ds(32 * kx, 32), pl.ds(128 * g, 128)] = high
                e_low[pl.ds(32 * kx, 32), pl.ds(128 * g, 128)] = low
        part = dot_nt(h[0], e_high[...])
        part += dot_nt(h[0], e_low[...])
        part += dot_nt(h[1], e_high[...])
        s2[f, b] = part.reshape(8, 32, 256)
        r2[f, b, right] = s2[f, b, right]
        for k in range(len(right_peers)):
            second(f, b, k).start()

    def along_z(f, b):
        all_second(f, b).wait_recv()
        for t in range(2):
            for g in range(2):
                arrays = [r2[f, b, 4 * g + i, :, pl.ds(128 * t, 128)] for i in range(4)]
                for i, array in enumerate(exchange_blocks(arrays, 32)):
                    high, low = split(array)
                    g_high[pl.ds(32 * (4 * t + i), 32), pl.ds(128 * g, 128)] = high
                    g_low[pl.ds(32 * (4 * t + i), 32), pl.ds(128 * g, 128)] = low
        part = dot_nn(g_high[...], h[0])
        part += dot_nn(g_low[...], h[0])
        part += dot_nn(g_high[...], h[1])
        modes[f] = part.reshape(8, 32, 256)

    def mixing(b):
        weights = [[mix[a, c] for c in range(F)] for a in range(F)]

        def plane(kx, carry):
            shift = sx[32 * left + 8 * b + kx]
            for part in range(4):
                rows = pl.ds(8 * part, 8)
                weight = 1.0 / (base[rows, :] + shift)
                other = 1.0 - weight
                old = [modes[a, kx, rows, :] for a in range(F)]
                for a in range(F):
                    mixed = weights[a][0] * old[0]
                    for c in range(1, F):
                        mixed += weights[a][c] * old[c]
                    out[a, 8 * b + kx, rows, :] = weight * old[a] + other * mixed
            return carry

        lax.fori_loop(0, 8, plane, 0)

    lax.fori_loop(0, F, along_x, 0)

    def send_rest(step, carry):
        send_first(step % F, step // F)
        return carry

    lax.fori_loop(F, F * BLOCKS, send_rest, 0)
    for copy in small[1:]:
        copy.wait()
    for ky in range(32):
        base[pl.ds(ky, 1), :] = 1.0 + (sz[...] + sy[32 * right + ky])

    def step(i, carry):
        @pl.when(i < F * BLOCKS)
        def _():
            along_y(i % F, i // F)

        @pl.when(i >= LAG)
        def _():
            j = i - LAG
            along_z(j % F, j // F)

            @pl.when(j % F == F - 1)
            def _():
                mixing(j // F)

        return carry

    lax.fori_loop(0, F * BLOCKS + LAG, step, 0)

    def finish(i, carry):
        all_first(i % F, i // F).wait_send()
        all_second(i % F, i // F).wait_send()
        return carry

    lax.fori_loop(0, F * BLOCKS, finish, 0)


def body(species, coupling, symbol_x, symbol_y, symbol_z):
    hbm = pl.BlockSpec(memory_space=pltpu.HBM)
    wide = basis_table(512)
    rows = np.arange(512).reshape(16, BLOCKS, 8).transpose(1, 0, 2).reshape(-1)
    tables_x = np.stack(halves(wide[rows]))
    tables = np.stack(halves(basis_table(256)))
    flat = jnp.transpose(species, (0, 2, 3, 1)).reshape(F * 512, 512)
    arrays = (flat, tables_x, tables, coupling, symbol_x, symbol_y, symbol_z.reshape(1, 256))
    return pl.pallas_call(
        kernel,
        out_shape=jax.ShapeDtypeStruct((F, 32, 32, 256), jnp.float32),
        in_specs=[hbm] * 7,
        out_specs=pl.BlockSpec(memory_space=pltpu.VMEM),
        scratch_shapes=[
            pltpu.VMEM((F * 4 * 512, 128), jnp.float32),
            pltpu.VMEM((2, 512, 512), jnp.bfloat16),
            pltpu.VMEM((2, 256, 256), jnp.bfloat16),
            pltpu.VMEM((512, 512), jnp.bfloat16),
            pltpu.VMEM((512, 512), jnp.bfloat16),
            pltpu.VMEM((F, BLOCKS, 16, 8, 512), jnp.float32),
            pltpu.VMEM((F, BLOCKS, 16, 8, 512), jnp.float32),
            pltpu.VMEM((512, 128), jnp.float32),
            pltpu.VMEM((256, 256), jnp.bfloat16),
            pltpu.VMEM((256, 256), jnp.bfloat16),
            pltpu.VMEM((F, BLOCKS, 8, 32, 256), jnp.float32),
            pltpu.VMEM((F, BLOCKS, 8, 32, 256), jnp.float32),
            pltpu.VMEM((256, 256), jnp.bfloat16),
            pltpu.VMEM((256, 256), jnp.bfloat16),
            pltpu.VMEM((F, 8, 32, 256), jnp.float32),
            pltpu.VMEM((32, 256), jnp.float32),
            pltpu.SMEM((F, F), jnp.float32),
            pltpu.SMEM((512,), jnp.float32),
            pltpu.SMEM((256,), jnp.float32),
            pltpu.VMEM((1, 256), jnp.float32),
            pltpu.SemaphoreType.DMA((F, 4)),
            pltpu.SemaphoreType.DMA((6,)),
            pltpu.SemaphoreType.DMA((F, BLOCKS)),
            pltpu.SemaphoreType.DMA((F, BLOCKS)),
            pltpu.SemaphoreType.DMA((F, BLOCKS)),
            pltpu.SemaphoreType.DMA((F, BLOCKS)),
        ],
        compiler_params=pltpu.CompilerParams(
            collective_id=0, has_side_effects=True, vmem_limit_bytes=40 * 2**20
        ),
        name="transform",
    )(*(pltpu.with_memory_space_constraint(a, pltpu.HBM) for a in arrays))


def solution(mesh):
    in_specs = (P(None, None, "left", "right"), P(), P(), P(), P())
    out_specs = P(None, "left", "right", None)
    return jax.shard_map(body, mesh=mesh, in_specs=in_specs, out_specs=out_specs, check_vma=False)
```

time: 102 us -> 68.7 us (0.67)
  other arithmetic: 14 us -> 0 us
  Pallas kernels: 79.9 us -> 66.6 us
  local copies, waits for them, and re-layouts: 7.37 us -> 2.02 us
    pallas_call x1, Pallas kernels: 79.9 us -> 66.6 us  [body(): pl.pallas_call(kernel, out_shape=jax.ShapeDtypeStruct((F, 32, 32, 256), j...]
    add x3 -> x0, other arithmetic: 11.7 us -> none  [the longest x2 11.6 us: body(): fields.append(weight * modes[a] + (1.0 - weight) * mixed)]
    another operation x1 -> x0, other arithmetic: 2.33 us -> none  [body(): return jnp.stack(fields)]
    slice x1 -> x0, local copies, waits for them, and re-layouts: 1.98 us -> none  [body(): mixed = sum((coupling[a, b] * modes[b] for b in range(F)))]
    unnamed x10 -> x1, local copies, waits for them, and re-layouts: 3.89 us -> 2.02 us
    dynamic_slice x2 -> x0, local copies, waits for them, and re-layouts: 1.5 us -> none  [the longest x1 0.75 us: body(): part_x = lax.dynamic_slice_in_dim(symbol_x, lax.axis_index('left') * 32, 32)]
where the time goes in v2:
time: 68.7 us; the launch traced here: 68.6 us
  Pallas kernels  66.6 us (97%)
  local copies, waits for them, and re-layouts  2.02 us (3%)
    pallas_call x1, Pallas kernels, body(): pl.pallas_call(kernel, out_shape=jax.ShapeDtypeStruct((F, 32, 32, 256), j...  66.6 us
    unnamed x1, local copies, waits for them, and re-layouts  2.02 us

profile of v2, /device:TPU:1, one launch (start us, length us, event | category | flops | bytes accessed | tf_op | source)
XLA Modules:
  0.0 68.6 jit_solution(9081052803670812498)
XLA Ops:
  0.0 66.6 %transform.1 = f32[4,32,32,256]{3,2,1,0:T(8,128)S(1)} custom-call(f32[2048,512]{1,0:T(8,128)} %bitcast.4, bf16[2,512,512]{2,1,0:T(8,128)(2,1)} %constant.4.clone.tables_x, bf16[2,256,256]{2,1,0:T(8,128)(2,1)} %constant.5.clone.tables, f32[4,4]{1,0:T(4,128)} %coupling.1, f32[512]{0:T(512)} %symbol_x.1, f32[256]{0:T(256)} %symbol_y.1, f32[1,256]{1,0:T(1,128)} %bitcast.5), custom_call_target="tpu_custom_call" | custom-call | tf_op jit(solution)/shard_map/transform/pallas_call | solution.py:275
  66.6 2.0 %copy.9 = f32[4,32,32,256]{3,2,1,0:T(8,128)} copy(f32[4,32,32,256]{3,2,1,0:T(8,128)S(1)} %transform.1) | data formatting | bytes 8388608

commit v3 on v2

--- a/solution.py
+++ b/solution.py
@@ -9,10 +9,11 @@
 MESH = pl.DeviceIdType.MESH
 F = 4
 BLOCKS = 4
-LAG = 2
-
-LEFT_STEPS = [(dz, dx) for dx in (0, 1, 3, 2) for dz in (1, 3, 2, 0) if (dz, dx) != (0, 0)]
-RIGHT_STEPS = [(dy, dc) for dy in (1, 3, 2, 0) for dc in (0, 1) if (dy, dc) != (0, 0)]
+LAG = 3
+AHEAD = 8
+
+LEFT_STEPS = [(dz, dx) for dx in (2, 1, 3, 0) for dz in (2, 1, 3, 0) if (dz, dx) != (0, 0)]
+RIGHT_STEPS = [(dy, dc) for dy in (2, 1, 3, 0) for dc in (0, 1) if (dy, dc) != (0, 0)]
 
 
 def basis_table(count):
@@ -138,40 +139,40 @@
         for k in range(len(left_peers)):
             first(f, b, k).start()
 
-    def along_x(f, carry):
+    def arrange(f):
         for t in range(4):
             load(f, t).wait()
         for t in range(4):
             for zi in range(32):
                 rows = grid[pl.ds((4 * f + t) * 512 + zi, 16, stride=32), :]
                 high, low = split(rows)
-                d_high[pl.ds(16 * zi, 16), pl.ds(128 * t, 128)] = high
-                d_low[pl.ds(16 * zi, 16), pl.ds(128 * t, 128)] = low
+                d_high[f, pl.ds(16 * zi, 16), pl.ds(128 * t, 128)] = high
+                d_low[f, pl.ds(16 * zi, 16), pl.ds(128 * t, 128)] = low
+
+    def along_x(f, p):
+        rows = pl.ds(pl.multiple_of(256 * p, 256), 256)
+        part = dot_nt(hx[0, rows, :], d_high[f])
+        part += dot_nt(hx[0, rows, :], d_low[f])
+        part += dot_nt(hx[1, rows, :], d_high[f])
+        s1[f, pl.ds(2 * p, 2)] = part.reshape(2, 16, 8, 512)
+        for i in range(2):
+            r1[f, 2 * p + i, left] = s1[f, 2 * p + i, left]
+
+    def opening(f, carry):
+        arrange(f)
 
         @pl.when(f == 0)
         def _():
             small[0].wait()
 
-        def pair(p, inner):
-            rows = pl.ds(pl.multiple_of(256 * p, 256), 256)
-            part = dot_nt(hx[0, rows, :], d_high[...])
-            part += dot_nt(hx[0, rows, :], d_low[...])
-            part += dot_nt(hx[1, rows, :], d_high[...])
-            s1[f, pl.ds(2 * p, 2)] = part.reshape(2, 16, 8, 512)
-            for i in range(2):
-                r1[f, 2 * p + i, left] = s1[f, 2 * p + i, left]
-
-            @pl.when(p == 0)
-            def _():
-                @pl.when(f == 0)
-                def _():
-                    pl.semaphore_wait(barrier, len(left_peers) + len(right_peers))
-
-                send_first(f, 0)
-
-            return inner
-
-        return lax.fori_loop(0, BLOCKS // 2, pair, carry)
+        along_x(f, 0)
+
+        @pl.when(f == 0)
+        def _():
+            pl.semaphore_wait(barrier, len(left_peers) + len(right_peers))
+
+        send_first(f, 0)
+        return carry
 
     def along_y(f, b):
         all_first(f, b).wait_recv()
@@ -226,17 +227,14 @@
 
         lax.fori_loop(0, 8, plane, 0)
 
-    lax.fori_loop(0, F, along_x, 0)
-
-    def send_rest(step, carry):
-        send_first(step % F, step // F)
+    lax.fori_loop(0, F, opening, 0)
+
+    def send_chunk(c, carry):
+        send_first(c % F, c // F)
         return carry
 
-    lax.fori_loop(F, F * BLOCKS, send_rest, 0)
-    for copy in small[1:]:
-        copy.wait()
-    for ky in range(32):
-        base[pl.ds(ky, 1), :] = 1.0 + (sz[...] + sy[32 * right + ky])
+    lax.fori_loop(F, AHEAD, send_chunk, 0)
+    small[1].wait()
 
     def step(i, carry):
         @pl.when(i < F * BLOCKS)
@@ -251,6 +249,21 @@
             @pl.when(j % F == F - 1)
             def _():
                 mixing(j // F)
+
+        @pl.when(i < F)
+        def _():
+            along_x(i, 1)
+
+        @pl.when(i + AHEAD < F * BLOCKS)
+        def _():
+            send_chunk(i + AHEAD, 0)
+
+        @pl.when(i == F)
+        def _():
+            for copy in small[2:]:
+                copy.wait()
+            for ky in range(32):
+                base[pl.ds(ky, 1), :] = 1.0 + (sz[...] + sy[32 * right + ky])
 
         return carry
 
@@ -281,8 +294,8 @@
             pltpu.VMEM((F * 4 * 512, 128), jnp.float32),
             pltpu.VMEM((2, 512, 512), jnp.bfloat16),
             pltpu.VMEM((2, 256, 256), jnp.bfloat16),
-            pltpu.VMEM((512, 512), jnp.bfloat16),
-            pltpu.VMEM((512, 512), jnp.bfloat16),
+            pltpu.VMEM((F, 512, 512), jnp.bfloat16),
+            pltpu.VMEM((F, 512, 512), jnp.bfloat16),
             pltpu.VMEM((F, BLOCKS, 16, 8, 512), jnp.float32),
             pltpu.VMEM((F, BLOCKS, 16, 8, 512), jnp.float32),
             pltpu.VMEM((512, 128), jnp.float32),

time: 68.7 us -> 65.9 us (0.959)
  Pallas kernels: 66.6 us -> 63.8 us
    pallas_call x1, Pallas kernels: 66.6 us -> 63.8 us  [body(): pl.pallas_call(kernel, out_shape=jax.ShapeDtypeStruct((F, 32, 32, 256), j...]
where the time goes in v3:
time: 65.9 us; the launch traced here: 65.8 us
  Pallas kernels  63.8 us (97%)
  local copies, waits for them, and re-layouts  2.02 us (3%)
    pallas_call x1, Pallas kernels, body(): pl.pallas_call(kernel, out_shape=jax.ShapeDtypeStruct((F, 32, 32, 256), j...  63.8 us
    unnamed x1, local copies, waits for them, and re-layouts  2.02 us

profile of v3, /device:TPU:1, one launch (start us, length us, event | category | flops | bytes accessed | tf_op | source)
XLA Modules:
  0.0 65.8 jit_solution(9111047211026700691)
XLA Ops:
  0.0 63.8 %transform.1 = f32[4,32,32,256]{3,2,1,0:T(8,128)S(1)} custom-call(f32[2048,512]{1,0:T(8,128)} %bitcast.4, bf16[2,512,512]{2,1,0:T(8,128)(2,1)} %constant.4.clone.tables_x, bf16[2,256,256]{2,1,0:T(8,128)(2,1)} %constant.5.clone.tables, f32[4,4]{1,0:T(4,128)} %coupling.1, f32[512]{0:T(512)} %symbol_x.1, f32[256]{0:T(256)} %symbol_y.1, f32[1,256]{1,0:T(1,128)} %bitcast.5), custom_call_target="tpu_custom_call" | custom-call | tf_op jit(solution)/shard_map/transform/pallas_call | solution.py:288
  63.8 2.0 %copy.9 = f32[4,32,32,256]{3,2,1,0:T(8,128)} copy(f32[4,32,32,256]{3,2,1,0:T(8,128)S(1)} %transform.1) | data formatting | bytes 8388608

commit v4 on v3

--- a/solution.py
+++ b/solution.py
@@ -11,6 +11,7 @@
 BLOCKS = 4
 LAG = 3
 AHEAD = 8
+LAST = F * BLOCKS - 1
 
 LEFT_STEPS = [(dz, dx) for dx in (2, 1, 3, 0) for dz in (2, 1, 3, 0) if (dz, dx) != (0, 0)]
 RIGHT_STEPS = [(dy, dc) for dy in (2, 1, 3, 0) for dc in (0, 1) if (dy, dc) != (0, 0)]
@@ -56,9 +57,23 @@
     return arrays
 
 
+def z_transform(pieces, h, g_high, g_low):
+    for t in range(2):
+        for g in range(2):
+            arrays = [pieces[4 * g + i, :, pl.ds(128 * t, 128)] for i in range(4)]
+            for i, array in enumerate(exchange_blocks(arrays, 32)):
+                high, low = split(array)
+                g_high[pl.ds(32 * (4 * t + i), 32), pl.ds(128 * g, 128)] = high
+                g_low[pl.ds(32 * (4 * t + i), 32), pl.ds(128 * g, 128)] = low
+    part = dot_nn(g_high[...], h[0])
+    part += dot_nn(g_low[...], h[0])
+    part += dot_nn(g_high[...], h[1])
+    return part.reshape(8, 32, 256)
+
+
 def kernel(
-    species, tables_x, tables, coupling, symbol_x, symbol_y, symbol_z, out,
-    grid, hx, h, d_high, d_low, s1, r1, d2, e_high, e_low, s2, r2, g_high, g_low, modes, base, mix, sx, sy, sz,
+    species, tables_x, tables, coupling, symbol_x, symbol_y, symbol_z, out, h, partial, slope, tail,
+    grid, hx, d_high, d_low, s1, r1, d2, e_high, e_low, s2, r2, g_high, g_low, modes, base, mix, sx, sy, sz,
     in_sem, h_sem, send1, recv1, send2, recv2,
 ):
     left, right = lax.axis_index("left"), lax.axis_index("right")
@@ -196,17 +211,7 @@
 
     def along_z(f, b):
         all_second(f, b).wait_recv()
-        for t in range(2):
-            for g in range(2):
-                arrays = [r2[f, b, 4 * g + i, :, pl.ds(128 * t, 128)] for i in range(4)]
-                for i, array in enumerate(exchange_blocks(arrays, 32)):
-                    high, low = split(array)
-                    g_high[pl.ds(32 * (4 * t + i), 32), pl.ds(128 * g, 128)] = high
-                    g_low[pl.ds(32 * (4 * t + i), 32), pl.ds(128 * g, 128)] = low
-        part = dot_nn(g_high[...], h[0])
-        part += dot_nn(g_low[...], h[0])
-        part += dot_nn(g_high[...], h[1])
-        modes[f] = part.reshape(8, 32, 256)
+        modes[f] = z_transform(r2.at[f, b], h, g_high, g_low)
 
     def mixing(b):
         weights = [[mix[a, c] for c in range(F)] for a in range(F)]
@@ -227,6 +232,32 @@
 
         lax.fori_loop(0, 8, plane, 0)
 
+    def prepare_last():
+        weights = [[mix[a, c] for c in range(F)] for a in range(F)]
+
+        def plane(kx, carry):
+            shift = sx[32 * left + 8 * (BLOCKS - 1) + kx]
+            for part in range(4):
+                rows = pl.ds(8 * part, 8)
+                weight = 1.0 / (base[rows, :] + shift)
+                other = 1.0 - weight
+                old = [modes[a, kx, rows, :] for a in range(F - 1)]
+                for a in range(F):
+                    mixed = weights[a][0] * old[0]
+                    for c in range(1, F - 1):
+                        mixed += weights[a][c] * old[c]
+                    first_terms = other * mixed
+                    last_term = weights[a][F - 1] * other
+                    if a < F - 1:
+                        partial[a, kx, rows, :] = weight * old[a] + first_terms
+                        slope[a, kx, rows, :] = last_term
+                    else:
+                        partial[a, kx, rows, :] = first_terms
+                        slope[a, kx, rows, :] = last_term + weight
+            return carry
+
+        lax.fori_loop(0, 8, plane, 0)
+
     lax.fori_loop(0, F, opening, 0)
 
     def send_chunk(c, carry):
@@ -244,6 +275,8 @@
         @pl.when(i >= LAG)
         def _():
             j = i - LAG
+            all_first(j % F, j // F).wait_send()
+            all_second(j % F, j // F).wait_send()
             along_z(j % F, j // F)
 
             @pl.when(j % F == F - 1)
@@ -267,33 +300,60 @@
 
         return carry
 
-    lax.fori_loop(0, F * BLOCKS + LAG, step, 0)
-
-    def finish(i, carry):
-        all_first(i % F, i // F).wait_send()
-        all_second(i % F, i // F).wait_send()
-        return carry
-
-    lax.fori_loop(0, F * BLOCKS, finish, 0)
+    lax.fori_loop(0, LAST + LAG, step, 0)
+    prepare_last()
+    all_first(F - 1, BLOCKS - 1).wait_send()
+    all_second(F - 1, BLOCKS - 1).wait_send()
+    all_second(F - 1, BLOCKS - 1).wait_recv()
+    tail[...] = r2[F - 1, BLOCKS - 1]
+
+
+def write_kernel(modes, h, partial, slope, tail, out, last, g_high, g_low, sems):
+    done = BLOCKS - 1
+    copies = [
+        pltpu.make_async_copy(modes.at[f, pl.ds(8 * b, 8)], out.at[f, pl.ds(8 * b, 8)], sems.at[f, b])
+        for f in range(F)
+        for b in range(done)
+    ]
+    for copy in copies:
+        copy.start()
+    last[F - 1] = z_transform(tail, h, g_high, g_low)
+    for kx in range(8):
+        for part in range(4):
+            rows = pl.ds(8 * part, 8)
+            old = last[F - 1, kx, rows, :]
+            for a in range(F):
+                last[a, kx, rows, :] = partial[a, kx, rows, :] + slope[a, kx, rows, :] * old
+    for f in range(F):
+        copies.append(pltpu.make_async_copy(last.at[f], out.at[f, pl.ds(8 * done, 8)], sems.at[f, done]))
+        copies[-1].start()
+    for copy in copies:
+        copy.wait()
 
 
 def body(species, coupling, symbol_x, symbol_y, symbol_z):
     hbm = pl.BlockSpec(memory_space=pltpu.HBM)
+    vmem = pl.BlockSpec(memory_space=pltpu.VMEM)
     wide = basis_table(512)
     rows = np.arange(512).reshape(16, BLOCKS, 8).transpose(1, 0, 2).reshape(-1)
     tables_x = np.stack(halves(wide[rows]))
     tables = np.stack(halves(basis_table(256)))
     flat = jnp.transpose(species, (0, 2, 3, 1)).reshape(F * 512, 512)
     arrays = (flat, tables_x, tables, coupling, symbol_x, symbol_y, symbol_z.reshape(1, 256))
-    return pl.pallas_call(
+    results = pl.pallas_call(
         kernel,
-        out_shape=jax.ShapeDtypeStruct((F, 32, 32, 256), jnp.float32),
+        out_shape=(
+            pltpu.VMEM((F, 8 * (BLOCKS - 1), 32, 256), jnp.float32),
+            pltpu.VMEM((2, 256, 256), jnp.bfloat16),
+            pltpu.VMEM((F, 8, 32, 256), jnp.float32),
+            pltpu.VMEM((F, 8, 32, 256), jnp.float32),
+            pltpu.VMEM((8, 32, 256), jnp.float32),
+        ),
         in_specs=[hbm] * 7,
-        out_specs=pl.BlockSpec(memory_space=pltpu.VMEM),
+        out_specs=[vmem] * 5,
         scratch_shapes=[
             pltpu.VMEM((F * 4 * 512, 128), jnp.float32),
             pltpu.VMEM((2, 512, 512), jnp.bfloat16),
-            pltpu.VMEM((2, 256, 256), jnp.bfloat16),
             pltpu.VMEM((F, 512, 512), jnp.bfloat16),
             pltpu.VMEM((F, 512, 512), jnp.bfloat16),
             pltpu.VMEM((F, BLOCKS, 16, 8, 512), jnp.float32),
@@ -323,6 +383,20 @@
         ),
         name="transform",
     )(*(pltpu.with_memory_space_constraint(a, pltpu.HBM) for a in arrays))
+    return pl.pallas_call(
+        write_kernel,
+        out_shape=jax.ShapeDtypeStruct((F, 32, 32, 256), jnp.float32),
+        in_specs=[vmem] * 5,
+        out_specs=hbm,
+        scratch_shapes=[
+            pltpu.VMEM((F, 8, 32, 256), jnp.float32),
+            pltpu.VMEM((256, 256), jnp.bfloat16),
+            pltpu.VMEM((256, 256), jnp.bfloat16),
+            pltpu.SemaphoreType.DMA((F, BLOCKS)),
+        ],
+        compiler_params=pltpu.CompilerParams(vmem_limit_bytes=4 * 2**20),
+        name="write",
+    )(*results)
 
 
 def solution(mesh):

time: 65.9 us -> 64.9 us (0.985)
  local copies, waits for them, and re-layouts: 2.02 us -> 0 us
  Pallas kernels: 63.8 us -> 64.8 us
    unnamed x1 -> x0, local copies, waits for them, and re-layouts: 2.02 us -> none
    pallas_call x1 -> x2, Pallas kernels: 63.8 us -> 64.8 us  [the longest x1 62.7 us: body(): pl.pallas_call(kernel, out_shape=(pltpu.VMEM((F, 8 * (BLOCKS - 1), 32, 25...]
where the time goes in v4:
time: 64.9 us; the launch traced here: 64.8 us
  Pallas kernels  64.8 us (100%)
    pallas_call x1, Pallas kernels, body(): pl.pallas_call(kernel, out_shape=(pltpu.VMEM((F, 8 * (BLOCKS - 1), 32, 25...  62.7 us
    pallas_call x1, Pallas kernels, body(): pl.pallas_call(write_kernel, out_shape=jax.ShapeDtypeStruct((F, 32, 32, 2...  2.16 us

profile of v4, /device:TPU:1, one launch (start us, length us, event | category | flops | bytes accessed | tf_op | source)
XLA Modules:
  0.0 64.8 jit_solution(96194341832079228)
XLA Ops:
  0.0 62.7 %transform.1 = (f32[4,24,32,256]{3,2,1,0:T(8,128)S(1)}, bf16[2,256,256]{2,1,0:T(8,128)(2,1)S(1)}, f32[4,8,32,256]{3,2,1,0:T(8,128)S(1)}, f32[4,8,32,256]{3,2,1,0:T(8,128)S(1)}, f32[8,32,256]{2,1,0:T(8,128)S(1)}) custom-call(f32[2048,512]{1,0:T(8,128)} %bitcast.4, bf16[2,512,512]{2,1,0:T(8,128)(2,1)} %constant.4.clone.tables_x, ...), custom_call_target="tpu_custom_call" | custom-call | tf_op jit(solution)/shard_map/transform/pallas_call | solution.py:343
  62.7 2.2 %write.1 = f32[4,32,32,256]{3,2,1,0:T(8,128)} custom-call(f32[4,24,32,256]{3,2,1,0:T(8,128)S(1)} %get-tuple-element.10.modes, bf16[2,256,256]{2,1,0:T(8,128)(2,1)S(1)} %get-tuple-element.11.h, f32[4,8,32,256]{3,2,1,0:T(8,128)S(1)} %get-tuple-element.12.partial, f32[4,8,32,256]{3,2,1,0:T(8,128)S(1)} %get-tuple-element.13.slope, ...), custom_call_target="tpu_custom_call" | custom-call | tf_op jit(solution)/shard_map/write/pallas_call | solution.py:386

commit v5 on v4

v5 whole, which is shorter than its diff:
```python
import jax
import jax.numpy as jnp
import numpy as np
from jax import lax
from jax.experimental import pallas as pl
from jax.experimental.pallas import tpu as pltpu
from jax.sharding import PartitionSpec as P

MESH = pl.DeviceIdType.MESH
F = 4
BLOCKS = 4
LAG = 5
AHEAD = 8
CHUNKS = 2 * F * BLOCKS
LAST = F * BLOCKS - 1

LEFT_STEPS = [(dz, dx) for dx in (2, 1, 3, 0) for dz in (2, 1, 3, 0) if (dz, dx) != (0, 0)]
RIGHT_STEPS = [(dy, dc) for dy in (2, 1, 3, 0) for dc in (0, 1) if (dy, dc) != (0, 0)]


def basis_table(count):
    rank = np.arange(count)
    angle = 2.0 * np.pi / count * (rank[:, None] * rank[None, :] % count)
    return ((np.cos(angle) + np.sin(angle)) * count**-0.5).astype(np.float32)


def halves(table):
    high = table.astype(jnp.bfloat16)
    low = (table - high.astype(np.float32)).astype(jnp.bfloat16)
    return high, low


def split(values):
    high = values.astype(jnp.bfloat16)
    return high, (values - high.astype(jnp.float32)).astype(jnp.bfloat16)


def dot_nt(a, b):
    return lax.dot_general(a, b, (((1,), (1,)), ((), ())), preferred_element_type=jnp.float32)


def dot_nn(a, b):
    return lax.dot_general(a, b, (((1,), (0,)), ((), ())), preferred_element_type=jnp.float32)


def gather_blocks(arrays, width):
    count = len(arrays)
    position = lax.broadcasted_iota(jnp.int32, arrays[0].shape, 1) // width
    moved = [arrays[-w % count] for w in range(count)]
    bit = 1
    while bit < count:
        odd = position // bit % 2 == 1
        moved = [jnp.where(odd, moved[(w - bit) % count], moved[w]) for w in range(count)]
        bit *= 2
    return [moved[0]] + [pltpu.roll(moved[w], 128 - width * w, 1) for w in range(1, count)]


def z_transform(pieces, h, g_high, g_low):
    for half in range(2):
        arrays = [pieces[half, i] for i in range(8)]
        for i, array in enumerate(gather_blocks(arrays, 16)):
            high, low = split(array)
            g_high[pl.ds(32 * i, 32), pl.ds(128 * half, 128)] = high
            g_low[pl.ds(32 * i, 32), pl.ds(128 * half, 128)] = low
    part = dot_nn(g_high[...], h[0])
    part += dot_nn(g_low[...], h[0])
    part += dot_nn(g_high[...], h[1])
    return part.reshape(8, 32, 256)


def kernel(
    species, tables_x, tables, tables_z, coupling, symbol_x, symbol_y, symbol_z, out, hz, partial, slope, tail,
    grid, hx, h, d_high, d_low, s1, r1, d2, e_high, e_low, s2, r2, g_high, g_low, modes, base, mix, sx, sy, sz,
    in_sem, h_sem, send1, recv1, send2, recv2,
):
    left, right = lax.axis_index("left"), lax.axis_index("right")
    z, x = left // 4, left % 4
    y, core = right // 2, right % 2
    left_peers = [lax.rem(z + dz, 4) * 4 + lax.rem(x + dx, 4) for dz, dx in LEFT_STEPS]
    right_peers = [lax.rem(y + dy, 4) * 2 + lax.rem(core + dc, 2) for dy, dc in RIGHT_STEPS]

    def load(f, t):
        return pltpu.make_async_copy(
            species.at[pl.ds(512 * f, 512), pl.ds(128 * t, 128)],
            grid.at[pl.ds((4 * f + t) * 512, 512)],
            in_sem.at[f],
        )

    def loaded(f):
        rows = pl.ds(2048 * f, 2048)
        pltpu.make_async_copy(grid.at[rows], grid.at[rows], in_sem.at[f]).wait()

    small = [
        pltpu.make_async_copy(a, b, h_sem.at[i])
        for i, (a, b) in enumerate(
            [(tables_x, hx), (tables, h), (tables_z, hz), (coupling, mix), (symbol_x, sx), (symbol_y, sy), (symbol_z, sz)]
        )
    ]
    for t in range(4):
        load(0, t).start()
    small[0].start()
    for f in range(1, F):
        for t in range(4):
            load(f, t).start()
    for copy in small[1:]:
        copy.start()

    barrier = pltpu.get_barrier_semaphore()
    for peer in left_peers:
        pl.semaphore_signal(barrier, inc=1, device_id=(peer, right), device_id_type=MESH)
    for peer in right_peers:
        pl.semaphore_signal(barrier, inc=1, device_id=(left, peer), device_id_type=MESH)

    def first(f, b, half, k):
        return pltpu.make_async_remote_copy(
            src_ref=s1.at[f, b, half, left_peers[k]],
            dst_ref=r1.at[f, b, half, left],
            send_sem=send1.at[b],
            recv_sem=recv1.at[f, b, half],
            device_id=(left_peers[k], right),
            device_id_type=MESH,
        )

    def second(f, b, half, k):
        return pltpu.make_async_remote_copy(
            src_ref=s2.at[f, b, half, right_peers[k]],
            dst_ref=r2.at[f, b, half, right],
            send_sem=send2.at[b],
            recv_sem=recv2.at[f, b],
            device_id=(left, right_peers[k]),
            device_id_type=MESH,
        )

    def all_first(f, b, half):
        return pltpu.make_async_remote_copy(
            src_ref=s1.at[f, b, half, pl.ds(0, 15)],
            dst_ref=r1.at[f, b, half, pl.ds(0, 15)],
            send_sem=send1.at[b],
            recv_sem=recv1.at[f, b, half],
            device_id=(left_peers[0], right),
            device_id_type=MESH,
        )

    def all_second(f, b):
        return pltpu.make_async_remote_copy(
            src_ref=s2.at[f, b, :, pl.ds(0, 7)],
            dst_ref=r2.at[f, b, :, pl.ds(0, 7)],
            send_sem=send2.at[b],
            recv_sem=recv2.at[f, b],
            device_id=(left, right_peers[0]),
            device_id_type=MESH,
        )

    def send_first(c):
        for k in range(len(left_peers)):
            first(c // 2 % F, c // (2 * F), c % 2, k).start()

    def sent(b):
        pltpu.make_async_remote_copy(
            src_ref=s1.at[:, b, :, pl.ds(0, 15)],
            dst_ref=r1.at[:, b, :, pl.ds(0, 15)],
            send_sem=send1.at[b],
            recv_sem=recv1.at[0, b, 0],
            device_id=(left_peers[0], right),
            device_id_type=MESH,
        ).wait_send()
        pltpu.make_async_remote_copy(
            src_ref=s2.at[:, b, :, pl.ds(0, 7)],
            dst_ref=r2.at[:, b, :, pl.ds(0, 7)],
            send_sem=send2.at[b],
            recv_sem=recv2.at[0, b],
            device_id=(left, right_peers[0]),
            device_id_type=MESH,
        ).wait_send()

    def arrange(f):
        loaded(f)
        for t in range(4):
            for zi in range(32):
                rows = grid[pl.ds((4 * f + t) * 512 + zi, 16, stride=32), :]
                high, low = split(rows)
                place = pl.multiple_of(16 * (zi // 8 * 8 + lax.rem(zi % 8 + left, 8)), 16)
                d_high[f, pl.ds(place, 16), pl.ds(128 * t, 128)] = high
                d_low[f, pl.ds(place, 16), pl.ds(128 * t, 128)] = low

    def along_x(f, p):
        rows = pl.ds(pl.multiple_of(256 * p, 256), 256)
        part = dot_nt(hx[0, rows, :], d_high[f])
        part += dot_nt(hx[0, rows, :], d_low[f])
        part += dot_nt(hx[1, rows, :], d_high[f])
        for half in range(2):
            s1[f, pl.ds(2 * p, 2), half] = part[:, 256 * half : 256 * half + 256].reshape(2, 16, 8, 256)
            for i in range(2):
                r1[f, 2 * p + i, half, left] = s1[f, 2 * p + i, half, left]

    def opening(f, carry):
        arrange(f)

        @pl.when(f == 0)
        def _():
            small[0].wait()

        along_x(f, 0)

        @pl.when(f == 0)
        def _():
            pl.semaphore_wait(barrier, len(left_peers) + len(right_peers))

        send_first(2 * f)
        send_first(2 * f + 1)
        return carry

    def along_y(f, b, half):
        all_first(f, b, half).wait_recv()
        for t in range(2):
            for g in range(2):
                arrays = [r1[f, b, half, 8 * g + i, :, pl.ds(128 * t, 128)] for i in range(8)]
                for i, array in enumerate(gather_blocks(arrays, 16)):
                    d2[pl.ds(128 * g + 8 * (8 * t + i), 8), :] = array
        for g in range(2):
            for kx in range(8):
                high, low = split(d2[pl.ds(128 * g + kx, 16, stride=8), :])
                place = pl.multiple_of(16 * lax.rem(kx + right, 8), 16)
                e_high[pl.ds(place, 16), pl.ds(128 * g, 128)] = high
                e_low[pl.ds(place, 16), pl.ds(128 * g, 128)] = low
        both = dot_nt(h[...].reshape(512, 256), e_high[...])
        part = both[:256] + both[256:] + dot_nt(h[0], e_low[...])
        s2[f, b, half] = part.reshape(8, 32, 128)
        r2[f, b, half, right] = s2[f, b, half, right]
        for k in range(len(right_peers)):
            second(f, b, half, k).start()

    def along_z(f, b):
        all_second(f, b).wait_recv()
        modes[b % 2, f] = z_transform(r2.at[f, b], hz, g_high, g_low)

    def mixing(b, kx):
        weights = [[mix[a, c] for c in range(F)] for a in range(F)]
        shift = sx[32 * left + 8 * b + kx]
        for part in range(4):
            rows = pl.ds(8 * part, 8)
            weight = 1.0 / (base[rows, :] + shift)
            other = 1.0 - weight
            old = [modes[b % 2, a, kx, rows, :] for a in range(F)]
            for a in range(F):
                mixed = weights[a][0] * old[0]
                for c in range(1, F):
                    mixed += weights[a][c] * old[c]
                out[a, 8 * b + kx, rows, :] = weight * old[a] + other * mixed

    def prepare_last():
        weights = [[mix[a, c] for c in range(F)] for a in range(F)]

        def plane(kx, carry):
            shift = sx[32 * left + 8 * (BLOCKS - 1) + kx]
            for part in range(4):
                rows = pl.ds(8 * part, 8)
                weight = 1.0 / (base[rows, :] + shift)
                other = 1.0 - weight
                old = [modes[(BLOCKS - 1) % 2, a, kx, rows, :] for a in range(F - 1)]
                for a in range(F):
                    mixed = weights[a][0] * old[0]
                    for c in range(1, F - 1):
                        mixed += weights[a][c] * old[c]
                    first_terms = other * mixed
                    last_term = weights[a][F - 1] * other
                    if a < F - 1:
                        partial[a, kx, rows, :] = weight * old[a] + first_terms
                        slope[a, kx, rows, :] = last_term
                    else:
                        partial[a, kx, rows, :] = first_terms
                        slope[a, kx, rows, :] = last_term + weight
            return carry

        lax.fori_loop(0, 8, plane, 0)

    lax.fori_loop(0, F, opening, 0)

    def send_chunk(c, carry):
        send_first(c)
        return carry

    lax.fori_loop(2 * F, AHEAD, send_chunk, 0)
    small[1].wait()

    def step(i, carry):
        @pl.when(i < CHUNKS)
        def _():
            along_y(i // 2 % F, i // (2 * F), i % 2)

        @pl.when(i < F)
        def _():
            along_x(i, 1)

        @pl.when(i + AHEAD < CHUNKS)
        def _():
            send_first(i + AHEAD)

        @pl.when(i == F)
        def _():
            for copy in small[2:]:
                copy.wait()
            for ky in range(32):
                base[pl.ds(ky, 1), :] = 1.0 + (sz[...] + sy[32 * right + ky])

        @pl.when(((i + LAG) % 2 == 1) & (i > LAG) & (i < 2 * LAST + LAG))
        def _():
            j = (i - LAG - 1) // 2
            along_z(j % F, j // F)

        plane = i - 2 * F - LAG

        @pl.when(plane >= 0)
        def _():
            mixing(plane // 8, plane % 8)

        return carry

    lax.fori_loop(0, CHUNKS + LAG, step, 0)
    prepare_last()
    for b in range(BLOCKS):
        sent(b)
    all_second(F - 1, BLOCKS - 1).wait_recv()
    tail[...] = r2[F - 1, BLOCKS - 1]


def write_kernel(modes, h, partial, slope, tail, out, last, g_high, g_low, sems):
    done = 8 * (BLOCKS - 1)
    copies = [
        pltpu.make_async_copy(modes.at[f], out.at[f, pl.ds(0, done)], sems.at[0, f]) for f in range(F)
    ]
    for copy in copies:
        copy.start()
    last[F - 1] = z_transform(tail, h, g_high, g_low)
    for kx in range(8):
        for part in range(4):
            rows = pl.ds(8 * part, 8)
            old = last[F - 1, kx, rows, :]
            for a in range(F):
                last[a, kx, rows, :] = partial[a, kx, rows, :] + slope[a, kx, rows, :] * old
    for f in range(F):
        copies.append(pltpu.make_async_copy(last.at[f], out.at[f, pl.ds(done, 8)], sems.at[1, f]))
        copies[-1].start()
    for copy in copies:
        copy.wait()


def body(species, coupling, symbol_x, symbol_y, symbol_z):
    hbm = pl.BlockSpec(memory_space=pltpu.HBM)
    vmem = pl.BlockSpec(memory_space=pltpu.VMEM)
    wide = basis_table(512)
    rows = np.arange(512).reshape(16, BLOCKS, 8).transpose(1, 0, 2).reshape(-1)
    tables_x = np.stack(halves(wide[rows]))
    tables = np.stack(halves(basis_table(256)))
    rows = np.arange(256).reshape(8, 2, 16).transpose(1, 0, 2).reshape(-1)
    tables_z = tables[:, rows]
    flat = jnp.transpose(species, (0, 2, 3, 1)).reshape(F * 512, 512)
    arrays = (flat, tables_x, tables, tables_z, coupling, symbol_x, symbol_y, symbol_z.reshape(1, 256))
    results = pl.pallas_call(
        kernel,
        out_shape=(
            pltpu.VMEM((F, 8 * (BLOCKS - 1), 32, 256), jnp.float32),
            pltpu.VMEM((2, 256, 256), jnp.bfloat16),
            pltpu.VMEM((F, 8, 32, 256), jnp.float32),
            pltpu.VMEM((F, 8, 32, 256), jnp.float32),
            pltpu.VMEM((2, 8, 32, 128), jnp.float32),
        ),
        in_specs=[hbm] * 8,
        out_specs=[vmem] * 5,
        scratch_shapes=[
            pltpu.VMEM((F * 4 * 512, 128), jnp.float32),
            pltpu.VMEM((2, 512, 512), jnp.bfloat16),
            pltpu.VMEM((2, 256, 256), jnp.bfloat16),
            pltpu.VMEM((F, 512, 512), jnp.bfloat16),
            pltpu.VMEM((F, 512, 512), jnp.bfloat16),
            pltpu.VMEM((F, BLOCKS, 2, 16, 8, 256), jnp.float32),
            pltpu.VMEM((F, BLOCKS, 2, 16, 8, 256), jnp.float32),
            pltpu.VMEM((256, 128), jnp.float32),
            pltpu.VMEM((128, 256), jnp.bfloat16),
            pltpu.VMEM((128, 256), jnp.bfloat16),
            pltpu.VMEM((F, BLOCKS, 2, 8, 32, 128), jnp.float32),
            pltpu.VMEM((F, BLOCKS, 2, 8, 32, 128), jnp.float32),
            pltpu.VMEM((256, 256), jnp.bfloat16),
            pltpu.VMEM((256, 256), jnp.bfloat16),
            pltpu.VMEM((2, F, 8, 32, 256), jnp.float32),
            pltpu.VMEM((32, 256), jnp.float32),
            pltpu.SMEM((F, F), jnp.float32),
            pltpu.SMEM((512,), jnp.float32),
            pltpu.SMEM((256,), jnp.float32),
            pltpu.VMEM((1, 256), jnp.float32),
            pltpu.SemaphoreType.DMA((F,)),
            pltpu.SemaphoreType.DMA((7,)),
            pltpu.SemaphoreType.DMA((BLOCKS,)),
            pltpu.SemaphoreType.DMA((F, BLOCKS, 2)),
            pltpu.SemaphoreType.DMA((BLOCKS,)),
            pltpu.SemaphoreType.DMA((F, BLOCKS)),
        ],
        compiler_params=pltpu.CompilerParams(
            collective_id=0, has_side_effects=True, vmem_limit_bytes=40 * 2**20
        ),
        name="transform",
    )(*(pltpu.with_memory_space_constraint(a, pltpu.HBM) for a in arrays))
    return pl.pallas_call(
        write_kernel,
        out_shape=jax.ShapeDtypeStruct((F, 32, 32, 256), jnp.float32),
        in_specs=[vmem] * 5,
        out_specs=hbm,
        scratch_shapes=[
            pltpu.VMEM((F, 8, 32, 256), jnp.float32),
            pltpu.VMEM((256, 256), jnp.bfloat16),
            pltpu.VMEM((256, 256), jnp.bfloat16),
            pltpu.SemaphoreType.DMA((2, F)),
        ],
        compiler_params=pltpu.CompilerParams(vmem_limit_bytes=4 * 2**20),
        name="write",
    )(*results)


def solution(mesh):
    in_specs = (P(None, None, "left", "right"), P(), P(), P(), P())
    out_specs = P(None, "left", "right", None)
    return jax.shard_map(body, mesh=mesh, in_specs=in_specs, out_specs=out_specs, check_vma=False)
```

time: 64.9 us -> 64.2 us (0.989)
  Pallas kernels: 64.8 us -> 64.1 us
where the time goes in v5:
time: 64.2 us; the launch traced here: 64.1 us
  Pallas kernels  64.1 us (100%)
    pallas_call x1, Pallas kernels, body(): pl.pallas_call(kernel, out_shape=(pltpu.VMEM((F, 8 * (BLOCKS - 1), 32, 25...  62 us
    pallas_call x1, Pallas kernels, body(): pl.pallas_call(write_kernel, out_shape=jax.ShapeDtypeStruct((F, 32, 32, 2...  2.07 us

profile of v5, /device:TPU:1, one launch (start us, length us, event | category | flops | bytes accessed | tf_op | source)
XLA Modules:
  0.0 64.1 jit_solution(14582561841056168064)
XLA Ops:
  0.0 62.0 %transform.1 = (f32[4,24,32,256]{3,2,1,0:T(8,128)S(1)}, bf16[2,256,256]{2,1,0:T(8,128)(2,1)S(1)}, f32[4,8,32,256]{3,2,1,0:T(8,128)S(1)}, f32[4,8,32,256]{3,2,1,0:T(8,128)S(1)}, f32[2,8,32,128]{3,2,1,0:T(8,128)S(1)}) custom-call(f32[2048,512]{1,0:T(8,128)} %bitcast.4, bf16[2,512,512]{2,1,0:T(8,128)(2,1)} %constant.6.clone.tables_x, ...), custom_call_target="tpu_custom_call" | custom-call | tf_op jit(solution)/shard_map/transform/pallas_call | solution.py:359
  62.1 2.1 %write.1 = f32[4,32,32,256]{3,2,1,0:T(8,128)} custom-call(f32[4,24,32,256]{3,2,1,0:T(8,128)S(1)} %get-tuple-element.10.modes, bf16[2,256,256]{2,1,0:T(8,128)(2,1)S(1)} %get-tuple-element.11.h, f32[4,8,32,256]{3,2,1,0:T(8,128)S(1)} %get-tuple-element.12.partial, f32[4,8,32,256]{3,2,1,0:T(8,128)S(1)} %get-tuple-element.13.slope, ...), custom_call_target="tpu_custom_call" | custom-call | tf_op jit(solution)/shard_map/write/pallas_call | solution.py:403

commit v6 on v5

--- a/solution.py
+++ b/solution.py
@@ -15,7 +15,7 @@
 LAST = F * BLOCKS - 1
 
 LEFT_STEPS = [(dz, dx) for dx in (2, 1, 3, 0) for dz in (2, 1, 3, 0) if (dz, dx) != (0, 0)]
-RIGHT_STEPS = [(dy, dc) for dy in (2, 1, 3, 0) for dc in (0, 1) if (dy, dc) != (0, 0)]
+RIGHT_STEPS = [(dy, dc) for dc in (0, 1) for dy in (2, 1, 3, 0) if (dy, dc) != (0, 0)]
 
 
 def basis_table(count):
@@ -79,6 +79,12 @@
     left_peers = [lax.rem(z + dz, 4) * 4 + lax.rem(x + dx, 4) for dz, dx in LEFT_STEPS]
     right_peers = [lax.rem(y + dy, 4) * 2 + lax.rem(core + dc, 2) for dy, dc in RIGHT_STEPS]
 
+    barrier = pltpu.get_barrier_semaphore()
+    for peer in left_peers:
+        pl.semaphore_signal(barrier, inc=1, device_id=(peer, right), device_id_type=MESH)
+    for peer in right_peers:
+        pl.semaphore_signal(barrier, inc=1, device_id=(left, peer), device_id_type=MESH)
+
     def load(f, t):
         return pltpu.make_async_copy(
             species.at[pl.ds(512 * f, 512), pl.ds(128 * t, 128)],
@@ -104,12 +110,6 @@
             load(f, t).start()
     for copy in small[1:]:
         copy.start()
-
-    barrier = pltpu.get_barrier_semaphore()
-    for peer in left_peers:
-        pl.semaphore_signal(barrier, inc=1, device_id=(peer, right), device_id_type=MESH)
-    for peer in right_peers:
-        pl.semaphore_signal(barrier, inc=1, device_id=(left, peer), device_id_type=MESH)
 
     def first(f, b, half, k):
         return pltpu.make_async_remote_copy(
@@ -226,9 +226,9 @@
         both = dot_nt(h[...].reshape(512, 256), e_high[...])
         part = both[:256] + both[256:] + dot_nt(h[0], e_low[...])
         s2[f, b, half] = part.reshape(8, 32, 128)
-        r2[f, b, half, right] = s2[f, b, half, right]
         for k in range(len(right_peers)):
             second(f, b, half, k).start()
+        r2[f, b, half, right] = s2[f, b, half, right]
 
     def along_z(f, b):
         all_second(f, b).wait_recv()
@@ -368,14 +368,14 @@
         in_specs=[hbm] * 8,
         out_specs=[vmem] * 5,
         scratch_shapes=[
-            pltpu.VMEM((F * 4 * 512, 128), jnp.float32),
+            pltpu.VMEM((F * 4 * 512 + 32, 128), jnp.float32),
             pltpu.VMEM((2, 512, 512), jnp.bfloat16),
             pltpu.VMEM((2, 256, 256), jnp.bfloat16),
             pltpu.VMEM((F, 512, 512), jnp.bfloat16),
             pltpu.VMEM((F, 512, 512), jnp.bfloat16),
             pltpu.VMEM((F, BLOCKS, 2, 16, 8, 256), jnp.float32),
             pltpu.VMEM((F, BLOCKS, 2, 16, 8, 256), jnp.float32),
-            pltpu.VMEM((256, 128), jnp.float32),
+            pltpu.VMEM((272, 128), jnp.float32),
             pltpu.VMEM((128, 256), jnp.bfloat16),
             pltpu.VMEM((128, 256), jnp.bfloat16),
             pltpu.VMEM((F, BLOCKS, 2, 8, 32, 128), jnp.float32),

time: 64.2 us -> 64.2 us (level)
  no operation moved by 1% of the time
where the time goes in v6:
time: 64.2 us; the launch traced here: 64.1 us
  Pallas kernels  64.1 us (100%)
    pallas_call x1, Pallas kernels, body(): pl.pallas_call(kernel, out_shape=(pltpu.VMEM((F, 8 * (BLOCKS - 1), 32, 25...  62 us
    pallas_call x1, Pallas kernels, body(): pl.pallas_call(write_kernel, out_shape=jax.ShapeDtypeStruct((F, 32, 32, 2...  2.07 us

profile of v6, /device:TPU:1, one launch (start us, length us, event | category | flops | bytes accessed | tf_op | source)
XLA Modules:
  0.0 64.1 jit_solution(12567118114221975542)
XLA Ops:
  0.0 62.0 %transform.1 = (f32[4,24,32,256]{3,2,1,0:T(8,128)S(1)}, bf16[2,256,256]{2,1,0:T(8,128)(2,1)S(1)}, f32[4,8,32,256]{3,2,1,0:T(8,128)S(1)}, f32[4,8,32,256]{3,2,1,0:T(8,128)S(1)}, f32[2,8,32,128]{3,2,1,0:T(8,128)S(1)}) custom-call(f32[2048,512]{1,0:T(8,128)} %bitcast.4, bf16[2,512,512]{2,1,0:T(8,128)(2,1)} %constant.6.clone.tables_x, ...), custom_call_target="tpu_custom_call" | custom-call | tf_op jit(solution)/shard_map/transform/pallas_call | solution.py:359
  62.0 2.1 %write.1 = f32[4,32,32,256]{3,2,1,0:T(8,128)} custom-call(f32[4,24,32,256]{3,2,1,0:T(8,128)S(1)} %get-tuple-element.10.modes, bf16[2,256,256]{2,1,0:T(8,128)(2,1)S(1)} %get-tuple-element.11.h, f32[4,8,32,256]{3,2,1,0:T(8,128)S(1)} %get-tuple-element.12.partial, f32[4,8,32,256]{3,2,1,0:T(8,128)S(1)} %get-tuple-element.13.slope, ...), custom_call_target="tpu_custom_call" | custom-call | tf_op jit(solution)/shard_map/write/pallas_call | solution.py:403

commit v7 on v6

--- a/solution.py
+++ b/solution.py
@@ -116,7 +116,7 @@
             src_ref=s1.at[f, b, half, left_peers[k]],
             dst_ref=r1.at[f, b, half, left],
             send_sem=send1.at[b],
-            recv_sem=recv1.at[f, b, half],
+            recv_sem=recv1.at[f, b % 2, half],
             device_id=(left_peers[k], right),
             device_id_type=MESH,
         )
@@ -126,7 +126,7 @@
             src_ref=s2.at[f, b, half, right_peers[k]],
             dst_ref=r2.at[f, b, half, right],
             send_sem=send2.at[b],
-            recv_sem=recv2.at[f, b],
+            recv_sem=recv2.at[f, b % 2],
             device_id=(left, right_peers[k]),
             device_id_type=MESH,
         )
@@ -136,7 +136,7 @@
             src_ref=s1.at[f, b, half, pl.ds(0, 15)],
             dst_ref=r1.at[f, b, half, pl.ds(0, 15)],
             send_sem=send1.at[b],
-            recv_sem=recv1.at[f, b, half],
+            recv_sem=recv1.at[f, b % 2, half],
             device_id=(left_peers[0], right),
             device_id_type=MESH,
         )
@@ -146,7 +146,7 @@
             src_ref=s2.at[f, b, :, pl.ds(0, 7)],
             dst_ref=r2.at[f, b, :, pl.ds(0, 7)],
             send_sem=send2.at[b],
-            recv_sem=recv2.at[f, b],
+            recv_sem=recv2.at[f, b % 2],
             device_id=(left, right_peers[0]),
             device_id_type=MESH,
         )
@@ -160,7 +160,7 @@
             src_ref=s1.at[:, b, :, pl.ds(0, 15)],
             dst_ref=r1.at[:, b, :, pl.ds(0, 15)],
             send_sem=send1.at[b],
-            recv_sem=recv1.at[0, b, 0],
+            recv_sem=recv1.at[0, b % 2, 0],
             device_id=(left_peers[0], right),
             device_id_type=MESH,
         ).wait_send()
@@ -168,7 +168,7 @@
             src_ref=s2.at[:, b, :, pl.ds(0, 7)],
             dst_ref=r2.at[:, b, :, pl.ds(0, 7)],
             send_sem=send2.at[b],
-            recv_sem=recv2.at[0, b],
+            recv_sem=recv2.at[0, b % 2],
             device_id=(left, right_peers[0]),
             device_id_type=MESH,
         ).wait_send()
@@ -391,9 +391,9 @@
             pltpu.SemaphoreType.DMA((F,)),
             pltpu.SemaphoreType.DMA((7,)),
             pltpu.SemaphoreType.DMA((BLOCKS,)),
-            pltpu.SemaphoreType.DMA((F, BLOCKS, 2)),
+            pltpu.SemaphoreType.DMA((F, 2, 2)),
             pltpu.SemaphoreType.DMA((BLOCKS,)),
-            pltpu.SemaphoreType.DMA((F, BLOCKS)),
+            pltpu.SemaphoreType.DMA((F, 2)),
         ],
         compiler_params=pltpu.CompilerParams(
             collective_id=0, has_side_effects=True, vmem_limit_bytes=40 * 2**20

time: 64.2 us -> 64 us (level)
  no operation moved by 1% of the time
where the time goes in v7:
time: 64 us; the launch traced here: 63.9 us
  Pallas kernels  63.9 us (100%)
    pallas_call x1, Pallas kernels, body(): pl.pallas_call(kernel, out_shape=(pltpu.VMEM((F, 8 * (BLOCKS - 1), 32, 25...  61.8 us
    pallas_call x1, Pallas kernels, body(): pl.pallas_call(write_kernel, out_shape=jax.ShapeDtypeStruct((F, 32, 32, 2...  2.07 us

profile of v7, /device:TPU:1, one launch (start us, length us, event | category | flops | bytes accessed | tf_op | source)
XLA Modules:
  0.0 63.9 jit_solution(2825204171768196102)
XLA Ops:
  0.0 61.8 %transform.1 = (f32[4,24,32,256]{3,2,1,0:T(8,128)S(1)}, bf16[2,256,256]{2,1,0:T(8,128)(2,1)S(1)}, f32[4,8,32,256]{3,2,1,0:T(8,128)S(1)}, f32[4,8,32,256]{3,2,1,0:T(8,128)S(1)}, f32[2,8,32,128]{3,2,1,0:T(8,128)S(1)}) custom-call(f32[2048,512]{1,0:T(8,128)} %bitcast.4, bf16[2,512,512]{2,1,0:T(8,128)(2,1)} %constant.6.clone.tables_x, ...), custom_call_target="tpu_custom_call" | custom-call | tf_op jit(solution)/shard_map/transform/pallas_call | solution.py:359
  61.8 2.1 %write.1 = f32[4,32,32,256]{3,2,1,0:T(8,128)} custom-call(f32[4,24,32,256]{3,2,1,0:T(8,128)S(1)} %get-tuple-element.10.modes, bf16[2,256,256]{2,1,0:T(8,128)(2,1)S(1)} %get-tuple-element.11.h, f32[4,8,32,256]{3,2,1,0:T(8,128)S(1)} %get-tuple-element.12.partial, f32[4,8,32,256]{3,2,1,0:T(8,128)S(1)} %get-tuple-element.13.slope, ...), custom_call_target="tpu_custom_call" | custom-call | tf_op jit(solution)/shard_map/write/pallas_call | solution.py:403

commit v8 on v6

--- a/solution.py
+++ b/solution.py
@@ -223,11 +223,16 @@
                 place = pl.multiple_of(16 * lax.rem(kx + right, 8), 16)
                 e_high[pl.ds(place, 16), pl.ds(128 * g, 128)] = high
                 e_low[pl.ds(place, 16), pl.ds(128 * g, 128)] = low
-        both = dot_nt(h[...].reshape(512, 256), e_high[...])
-        part = both[:256] + both[256:] + dot_nt(h[0], e_low[...])
-        s2[f, b, half] = part.reshape(8, 32, 128)
-        for k in range(len(right_peers)):
-            second(f, b, half, k).start()
+        for dy in (2, 1, 3, 0):
+            chip = lax.rem(y + dy, 4)
+            rows = pl.ds(pl.multiple_of(64 * chip, 64), 64)
+            part = dot_nt(h[0, rows, :], e_high[...])
+            part += dot_nt(h[0, rows, :], e_low[...])
+            part += dot_nt(h[1, rows, :], e_high[...])
+            s2[f, b, half, pl.ds(2 * chip, 2)] = part.reshape(2, 32, 128)
+            for k, (step_y, _) in enumerate(RIGHT_STEPS):
+                if step_y == dy:
+                    second(f, b, half, k).start()
         r2[f, b, half, right] = s2[f, b, half, right]
 
     def along_z(f, b):

time: 64.2 us -> 67.3 us (1.048)
  Pallas kernels: 64.1 us -> 67.2 us
    pallas_call x1, Pallas kernels: 62 us -> 65.1 us  [body(): pl.pallas_call(kernel, out_shape=(pltpu.VMEM((F, 8 * (BLOCKS - 1), 32, 25...]
where the time goes in v8:
time: 67.3 us; the launch traced here: 67.2 us
  Pallas kernels  67.2 us (100%)
    pallas_call x1, Pallas kernels, body(): pl.pallas_call(kernel, out_shape=(pltpu.VMEM((F, 8 * (BLOCKS - 1), 32, 25...  65.1 us
    pallas_call x1, Pallas kernels, body(): pl.pallas_call(write_kernel, out_shape=jax.ShapeDtypeStruct((F, 32, 32, 2...  2.07 us

profile of v8, /device:TPU:1, one launch (start us, length us, event | category | flops | bytes accessed | tf_op | source)
XLA Modules:
  0.0 67.2 jit_solution(16885085442047806148)
XLA Ops:
  0.0 65.1 %transform.1 = (f32[4,24,32,256]{3,2,1,0:T(8,128)S(1)}, bf16[2,256,256]{2,1,0:T(8,128)(2,1)S(1)}, f32[4,8,32,256]{3,2,1,0:T(8,128)S(1)}, f32[4,8,32,256]{3,2,1,0:T(8,128)S(1)}, f32[2,8,32,128]{3,2,1,0:T(8,128)S(1)}) custom-call(f32[2048,512]{1,0:T(8,128)} %bitcast.4, bf16[2,512,512]{2,1,0:T(8,128)(2,1)} %constant.6.clone.tables_x, ...), custom_call_target="tpu_custom_call" | custom-call | tf_op jit(solution)/shard_map/transform/pallas_call | solution.py:364
  65.1 2.1 %write.1 = f32[4,32,32,256]{3,2,1,0:T(8,128)} custom-call(f32[4,24,32,256]{3,2,1,0:T(8,128)S(1)} %get-tuple-element.10.modes, bf16[2,256,256]{2,1,0:T(8,128)(2,1)S(1)} %get-tuple-element.11.h, f32[4,8,32,256]{3,2,1,0:T(8,128)S(1)} %get-tuple-element.12.partial, f32[4,8,32,256]{3,2,1,0:T(8,128)S(1)} %get-tuple-element.13.slope, ...), custom_call_target="tpu_custom_call" | custom-call | tf_op jit(solution)/shard_map/write/pallas_call | solution.py:408
